TPU v7x, 32 devices: a whole 2x2x4 slice. The times are simulated.
32 devices in a mesh: role: 2 (over core), shard: 16 (over z, y, x).
Axes of the slice: x: 2, y: 2, z: 4, core: 2. Of those that a mesh axis runs over, the one named last changes fastest.
Arguments:
- history: bfloat16 [256, 640, 128], P(None, ('role', 'shard')), may hold values from -20 to 20
- event_cat: int32 [256, 640], P(None, ('role', 'shard')), may hold values from 0 to 1023, as said below
- candidates: bfloat16 [256, 200, 128], P(('role', 'shard')), may hold values from -9 to 9
- cand_cat: int32 [256, 200], P(('role', 'shard')), may hold values from 0 to 1023, as said below
- w_input: bfloat16 [256, 512], replicated, may hold values from -0.375 to 0.375
- w_output: bfloat16 [512, 128], replicated, may hold values from -0.25 to 0.25
Outputs:
- interest_features: bfloat16 [256, 200, 128], P(('role', 'shard'))
Inputs may be any that keep to these rules, and one draw needn't show every extreme that they name: `event_cat`: in each aligned block of 20 events of one user, at most 8 events have a category that some candidate of that user has; users 2 i and 2 i + 1 have exactly 8 such events together in every block; every user has a block with exactly 8. `cand_cat`: the candidates of one user carry at most 8 distinct categories.
All inputs are finite; a program needn't handle non-finite values.
Results may differ from a plain program's by a relative error of at most 0.0095.
Values may be sent and summed in bfloat16 or wider, within the bound.
No kernel may reach another device: no remote copies, remote signals or barrier semaphores. Data moves between devices by JAX's collectives and lax.ppermute only.
A program may use at most 64 MiB of HBM per device.

v0:
```python
import math

import jax
import jax.numpy as jnp
from jax import lax
from jax.sharding import PartitionSpec as P

HEADS = 4
CAP = 8


def attend(queries, event_keys, allowed):
    group = queries.shape[0]
    count = queries.shape[1]
    width = queries.shape[2]
    head_size = width // HEADS
    query_heads = queries.reshape(group, count, HEADS, head_size)
    key_heads = event_keys.reshape(group, -1, HEADS, head_size)
    scores = jnp.einsum(
        "gchk,gshk->ghcs", query_heads, key_heads, preferred_element_type=jnp.float32
    ) * head_size ** (-0.5)
    scores = jnp.where(allowed[:, None, None, :], scores, -1e30)
    row_max = jnp.max(scores, axis=-1, keepdims=True)
    expo = jnp.exp(scores - row_max)
    total = jnp.sum(expo, axis=-1, keepdims=True)
    weights = (expo / total).astype(jnp.bfloat16)
    interest = jnp.einsum("ghcs,gshk->gchk", weights, key_heads, preferred_element_type=jnp.float32)
    return interest.reshape(group, count, width).astype(jnp.bfloat16)


def local(history, event_cat, candidates, cand_cat, w_input, w_output):
    wanted = lax.all_gather(cand_cat, ("role", "shard"), axis=0, tiled=True)
    hits = jnp.any(event_cat[:, :, None] == wanted[:, None, :], axis=-1)
    slot_rank = jnp.cumsum(hits.astype(jnp.int32), axis=1) - 1
    places = jnp.arange(CAP, dtype=jnp.int32)
    place_values = places.astype(jnp.float32)
    own_users = candidates.shape[0]
    cand_count = candidates.shape[1]
    width = candidates.shape[2]
    rows = own_users * cand_count
    cand_part = jnp.dot(
        candidates.reshape(rows, width), w_input[:width], preferred_element_type=jnp.float32
    )
    hit_counts = jnp.sum(hits.astype(jnp.int32), axis=1)
    pair_counts = hit_counts.reshape(-1, 2)
    start = jnp.stack([jnp.zeros_like(pair_counts[:, 0]), pair_counts[:, 0]], axis=1).reshape(-1)
    shifted = slot_rank + start[:, None]
    selector = (hits[:, None, :] & (shifted[:, None, :] == places[None, :, None])).astype(
        jnp.bfloat16
    )
    spread = jnp.einsum("use,ued->usd", selector, history, preferred_element_type=jnp.float32)
    packed = jnp.sum(spread.reshape(-1, 2, CAP, width), axis=1).astype(jnp.bfloat16)
    received, counts_in = (
        lax.all_to_all(packed, ("role", "shard"), split_axis=0, concat_axis=1, tiled=True),
        lax.all_to_all(
            pair_counts.astype(jnp.bfloat16),
            ("role", "shard"),
            split_axis=0,
            concat_axis=1,
            tiled=True,
        ),
    )
    half = own_users // 2
    counts_in = counts_in.astype(jnp.float32).reshape(half, -1, 2)
    lead = counts_in[:, :, 0][:, :, None]
    follow = counts_in[:, :, 1][:, :, None]
    lead_use = place_values[None, None, :] < lead
    follow_use = (place_values[None, None, :] >= lead) & (
        place_values[None, None, :] < lead + follow
    )
    usable = jnp.stack([lead_use, follow_use], axis=1).reshape(own_users, -1)
    received = jnp.repeat(received, 2, axis=0)
    group = math.gcd(own_users, 4)
    packs = own_users // group

    def one_pack(pieces):
        return attend(pieces[0], pieces[1], pieces[2])

    interest = lax.map(
        one_pack,
        (
            candidates.reshape(packs, group, cand_count, width),
            received.reshape(packs, group, -1, width),
            usable.reshape(packs, group, -1),
        ),
    )
    interest = interest.reshape(rows, width)
    hidden = cand_part + jnp.dot(interest, w_input[width:], preferred_element_type=jnp.float32)
    hidden = jax.nn.silu(hidden).astype(jnp.bfloat16)
    result = jnp.dot(hidden, w_output, preferred_element_type=jnp.float32).astype(jnp.bfloat16)
    return result.reshape(own_users, cand_count, width)


def solution(mesh):
    placed = (
        P(None, ("role", "shard"), None),
        P(None, ("role", "shard")),
        P(("role", "shard"), None, None),
        P(("role", "shard"), None),
        P(),
        P(),
    )
    return jax.shard_map(
        local,
        mesh=mesh,
        in_specs=placed,
        out_specs=P(("role", "shard"), None, None),
        check_vma=False,
    )
```

profile of v0, /device:TPU:0, one launch (start us, length us, event | category | flops | bytes accessed | tf_op | source)
XLA Modules:
  0.0 117.8 jit_solution(6758111273097364746)
XLA Ops:
  0.0 0.0 copy-start
  0.0 71.8 %all_gather.3 = s32[256,200]{1,0:T(8,128)S(1)} all-gather(s32[8,200]{1,0:T(8,128)} %param.11), channel_id=1, replica_groups=mesh['role'=2,'shard'=16] {'role','shard'}, dimensions={0}, use_global_device_ids=true | all-gather | bytes 211200 | tf_op jit(solution)/shard_map/all_gather | solution.py:32
  71.8 0.1 copy.34
  71.9 1.5 %compare_reduce_fusion = pred[256,20]{0,1:T(8,128)(4,1)S(1)} fusion(s32[256,200]{0,1:T(8,128)S(1)} %copy.34, s32[256,20]{0,1:T(8,128)} %param.9), kind=kLoop, calls=%fused_computation.17 | loop fusion | flops 2042880 | bytes 230400 | tf_op jit(solution)/shard_map/reduce_or | solution.py:33
  73.5 0.2 convert_element_type.66
  73.7 0.9 copy.40
  74.6 2.5 %all-to-all-start.1 = ((bf16[32,4,2]{1,2,0:T(2,128)(2,1)}), bf16[32,4,2]{1,2,0:T(2,128)(2,1)S(1)}, u32[]{:S(2)}, u32[]{:S(2)}) async-start(bf16[32,4,2]{1,2,0:T(2,128)(2,1)} %copy.40), calls=%async_computation.1 | async-start | bytes 32768 | tf_op jit(solution)/shard_map/all_to_all | solution.py:55
  77.1 0.1 reshape.92
  77.2 0.1 copy.35
  77.4 0.1 stack.8
  77.5 0.1 add.34
  77.6 0.0 copy-start.1
  77.7 0.1 copy.36
  77.8 3.3 %fusion.23 = f32[1600,512]{1,0:T(8,128)} fusion(bf16[1600,128]{1,0:T(8,128)(2,1)} %bitcast.55, bf16[256,512]{1,0:T(8,128)(2,1)} %param.12), kind=kOutput, calls=%fused_computation.30 | convolution fusion | flops 209715200 | bytes 3817472 | tf_op jit(solution)/shard_map/dot_general | solution.py:41
  81.1 0.0 copy-done
  81.1 2.0 %bitcast_reduce_fusion = bf16[128,8,128]{2,1,0:T(8,128)(2,1)} fusion(bf16[256,20,128]{2,0,1:T(8,128)(2,1)S(1)} %copy-done, s32[256,20]{1,0:T(8,128)S(1)} %copy.36, pred[256,20]{1,0:T(8,128)(4,1)S(1)} %copy.35), kind=kOutput, calls=%fused_computation.23 | convolution fusion | flops 10698752 | bytes 1598464 | tf_op jit(solution)/shard_map/use,ued->usd/dot_general | solution.py:51
  83.1 0.0 copy-done.1
  83.1 0.2 copy.44
  83.3 0.9 all-to-all-done.1
  84.2 5.0 %all-to-all-start = ((bf16[128,8,128]{2,1,0:T(8,128)(2,1)}), bf16[128,8,128]{2,1,0:T(8,128)(2,1)S(1)}, u32[]{:S(2)}, u32[]{:S(2)}) async-start(bf16[128,8,128]{2,1,0:T(8,128)(2,1)} %bitcast_reduce_fusion), calls=%async_computation | async-start | bytes 524288 | tf_op jit(solution)/shard_map/all_to_all | solution.py:54
  89.3 0.1 copy.41
  89.3 0.1 copy.42
  89.4 0.1 broadcast_compare_fusion
  89.5 0.1 copy.43
  89.6 0.1 reshape_reshape.7
  89.8 10.6 %all-to-all-done = bf16[128,8,128]{2,1,0:T(8,128)(2,1)S(1)} async-done(((bf16[128,8,128]{2,1,0:T(8,128)(2,1)}), bf16[128,8,128]{2,1,0:T(8,128)(2,1)S(1)}, u32[]{:S(2)}, u32[]{:S(2)}) %all-to-all-start) | async-done | bytes 262176 | tf_op jit(solution)/shard_map/all_to_all | solution.py:54
  100.4 0.1 copy.39
  100.6 0.0 copy-start.2
  100.6 0.0 copy-start.3
  100.7 12.9 %while.10 = (s32[]{:T(128)}, bf16[2,4,200,128]{3,2,1,0:T(8,128)(2,1)}, bf16[2,4,256,128]{2,3,1,0:T(8,128)(2,1)S(1)}, pred[2,4,256]{2,1,0:T(4,128)(4,1)S(1)}, bf16[2,4,200,128]{2,3,1,0:T(8,128)(2,1)S(1)}, /*index=5*/s32[]{:T(128)}) while((s32[]{:T(128)}, bf16[2,4,200,128]{3,2,1,0:T(8,128)(2,1)}, bf16[2,4,256,128]{2,3,1,0:T(8,128)(2,1)S(1)}, ...), condition=%wide.region_7.8_spmd, body=%wide.region_4.7_spmd.sunk | while | flops 109875456 | bytes 9269841 | solution.py:79
  100.8 2.9 %fusion.44 = (f32[4,4,200]{2,1,0:T(4,128)S(1)}, f32[4,4,200,256]{3,2,1,0:T(8,128)}) fusion(pred[4,256]{1,0:T(4,128)(4,1)S(1)} %dynamic-slice_bitcast_fusion.2, bf16[4,200,4,32]{1,3,2,0:T(8,128)(2,1)S(1)} %bitcast.51, bf16[4,256,4,32]{1,3,2,0:T(8,128)(2,1)S(1)} %bitcast.49), kind=kOutput, calls=%fused_computation.41.clone.1 | convolution fusion | flops 55705856 | bytes 3757568 | tf_op jit(solution)/shard_map/while/body/eval_jaxpr/sub | solution.py:24
  103.6 2.6 %fusion.45 = bf16[4,4,32,200]{3,2,1,0:T(8,128)(2,1)S(1)} fusion(bf16[4,256,4,32]{1,3,2,0:T(8,128)(2,1)S(1)} %bitcast.50, f32[4,4,200,256]{3,2,1,0:T(8,128)} %get-tuple-element.82, f32[4,4,200]{2,1,0:T(4,128)S(1)} %get-tuple-element.83), kind=kOutput, calls=%fused_computation.9.clone.1 | convolution fusion | flops 54169600 | bytes 3756544 | tf_op jit(solution)/shard_map/while/body/eval_jaxpr/ghcs,gshk->gchk/dot_general | solution.py:27
  106.2 0.2 copy.55
  106.4 0.7 constant_dynamic-update-slice_fusion.2
  107.2 2.9 %fusion.44 = (f32[4,4,200]{2,1,0:T(4,128)S(1)}, f32[4,4,200,256]{3,2,1,0:T(8,128)}) fusion(pred[4,256]{1,0:T(4,128)(4,1)S(1)} %dynamic-slice_bitcast_fusion.2, bf16[4,200,4,32]{1,3,2,0:T(8,128)(2,1)S(1)} %bitcast.51, bf16[4,256,4,32]{1,3,2,0:T(8,128)(2,1)S(1)} %bitcast.49), kind=kOutput, calls=%fused_computation.41.clone.1 | convolution fusion | flops 55705856 | bytes 3757568 | tf_op jit(solution)/shard_map/while/body/eval_jaxpr/sub | solution.py:24
  110.1 2.6 %fusion.45 = bf16[4,4,32,200]{3,2,1,0:T(8,128)(2,1)S(1)} fusion(bf16[4,256,4,32]{1,3,2,0:T(8,128)(2,1)S(1)} %bitcast.50, f32[4,4,200,256]{3,2,1,0:T(8,128)} %get-tuple-element.82, f32[4,4,200]{2,1,0:T(4,128)S(1)} %get-tuple-element.83), kind=kOutput, calls=%fused_computation.9.clone.1 | convolution fusion | flops 54169600 | bytes 3756544 | tf_op jit(solution)/shard_map/while/body/eval_jaxpr/ghcs,gshk->gchk/dot_general | solution.py:27
  112.7 0.2 copy.55
  112.9 0.7 constant_dynamic-update-slice_fusion.2
  113.6 0.0 copy-done.2
  113.6 0.0 copy-done.3
  113.6 4.2 %convolution_convert_fusion = bf16[1600,128]{1,0:T(8,128)(2,1)} fusion(bf16[512,128]{1,0:T(8,128)(2,1)S(1)} %copy-done.3, f32[1600,512]{1,0:T(8,128)} %fusion.23, bf16[1600,128]{1,0:T(8,128)(2,1)} %bitcast.61, bf16[256,512]{1,0:T(8,128)(2,1)S(1)} %copy-done.2), kind=kOutput, calls=%fused_computation.20 | convolution fusion | flops 424550400 | bytes 4358144 | tf_op jit(solution)/shard_map/dot_general | solution.py:90
  (18 shorter events, 0.3 us)
Async XLA Ops:
  0.0 81.1 %copy-start = (bf16[256,20,128]{2,0,1:T(8,128)(2,1)S(1)}, bf16[256,20,128]{2,0,1:T(8,128)(2,1)}, u32[]{:S(2)}) copy-start(bf16[256,20,128]{2,0,1:T(8,128)(2,1)} %param.8) | copy-start | bytes 3932164
  74.6 9.6 %all-to-all-start.1 = ((bf16[32,4,2]{1,2,0:T(2,128)(2,1)}), bf16[32,4,2]{1,2,0:T(2,128)(2,1)S(1)}, u32[]{:S(2)}, u32[]{:S(2)}) async-start(bf16[32,4,2]{1,2,0:T(2,128)(2,1)} %copy.40), calls=%async_computation.1 | async-start | bytes 32768 | tf_op jit(solution)/shard_map/all_to_all | solution.py:55
  77.6 5.5 %copy-start.1 = (bf16[8,200,128]{2,1,0:T(8,128)(2,1)S(1)}, bf16[8,200,128]{2,1,0:T(8,128)(2,1)}, u32[]{:S(2)}) copy-start(bf16[8,200,128]{2,1,0:T(8,128)(2,1)} %param.10) | copy-start | bytes 1228804
  84.2 16.2 %all-to-all-start = ((bf16[128,8,128]{2,1,0:T(8,128)(2,1)}), bf16[128,8,128]{2,1,0:T(8,128)(2,1)S(1)}, u32[]{:S(2)}, u32[]{:S(2)}) async-start(bf16[128,8,128]{2,1,0:T(8,128)(2,1)} %bitcast_reduce_fusion), calls=%async_computation | async-start | bytes 524288 | tf_op jit(solution)/shard_map/all_to_all | solution.py:54
  100.6 12.9 %copy-start.2 = (bf16[256,512]{1,0:T(8,128)(2,1)S(1)}, bf16[256,512]{1,0:T(8,128)(2,1)}, u32[]{:S(2)}) copy-start(bf16[256,512]{1,0:T(8,128)(2,1)} %param.12) | copy-start | bytes 786436
  100.6 12.9 %copy-start.3 = (bf16[512,128]{1,0:T(8,128)(2,1)S(1)}, bf16[512,128]{1,0:T(8,128)(2,1)}, u32[]{:S(2)}) copy-start(bf16[512,128]{1,0:T(8,128)(2,1)} %param.13) | copy-start | bytes 393220
where the time goes:
time: 118 us
  blocking collectives  71.8 us (61%)
  matrix products  20.5 us (17%)
  waiting for transfers between devices  11.5 us (10%)
  starting transfers between devices  7.46 us (6%)
  local copies, waits for them, and re-layouts  4.56 us (4%)
  other arithmetic  1.77 us (2%)
    all_gather x1, blocking collectives, local(): wanted = lax.all_gather(cand_cat, ('role', 'shard'), axis=0, tiled=True)  71.8 us
    all_to_all x1, waiting for transfers between devices, local(): lax.all_to_all(packed, ('role', 'shard'), split_axis=0, concat_axis=1, ti...  10.6 us
    sub x2, matrix products, attend(): expo = jnp.exp(scores - row_max)  5.73 us
    dot_general x2, matrix products, attend(): jnp.einsum('ghcs,gshk->gchk', weights, key_heads, preferred_element_type=...  5.23 us
    all_to_all x1, starting transfers between devices, local(): lax.all_to_all(packed, ('role', 'shard'), split_axis=0, concat_axis=1, ti...  4.97 us
    dot_general x1, matrix products, local(): jnp.dot(hidden, w_output, preferred_element_type=jnp.float32)  4.21 us
    dot_general x1, matrix products, local(): jnp.dot(candidates.reshape(rows, width), w_input[:width], preferred_eleme...  3.28 us
    all_to_all x1, starting transfers between devices, local(): lax.all_to_all(pair_counts.astype(jnp.bfloat16), ('role', 'shard'), split...  2.49 us
  transfers between devices with their start and end apart: 2, of which 2 were waited for; matrix products, arithmetic and copies ran while one was open for 6% of the time, Pallas kernels for 0%

commit v1 on v0

--- a/solution.py
+++ b/solution.py
@@ -7,6 +7,18 @@
 
 HEADS = 4
 CAP = 8
+QCAT = 8
+
+
+def distinct_categories(cand_cat):
+    beyond = jnp.iinfo(jnp.int32).max
+    current = jnp.min(cand_cat, axis=1)
+    found = [current]
+    for _ in range(QCAT - 1):
+        following = jnp.min(jnp.where(cand_cat > current[:, None], cand_cat, beyond), axis=1)
+        current = jnp.where(following == beyond, current, following)
+        found.append(current)
+    return jnp.stack(found, axis=1)
 
 
 def attend(queries, event_keys, allowed):
@@ -29,7 +41,15 @@
 
 
 def local(history, event_cat, candidates, cand_cat, w_input, w_output):
-    wanted = lax.all_gather(cand_cat, ("role", "shard"), axis=0, tiled=True)
+    devices = lax.axis_size(("role", "shard"))
+    own_wanted = distinct_categories(cand_cat).reshape(1, 1, -1)
+    wanted = lax.all_to_all(
+        jnp.broadcast_to(own_wanted, (devices, 1, own_wanted.shape[2])),
+        ("role", "shard"),
+        split_axis=0,
+        concat_axis=0,
+        tiled=True,
+    ).reshape(-1, QCAT)
     hits = jnp.any(event_cat[:, :, None] == wanted[:, None, :], axis=-1)
     slot_rank = jnp.cumsum(hits.astype(jnp.int32), axis=1) - 1
     places = jnp.arange(CAP, dtype=jnp.int32)

time: 118 us -> 66.9 us (0.57)
  blocking collectives: 71.8 us -> 0 us
  waiting for transfers between devices: 11.5 us -> 18.9 us
  other arithmetic: 1.77 us -> 8.15 us
  starting transfers between devices: 7.46 us -> 12.4 us
  local copies, waits for them, and re-layouts: 4.56 us -> 5.91 us
    all_gather x1 -> x0, blocking collectives: 71.8 us -> none  [local(): wanted = lax.all_gather(cand_cat, ('role', 'shard'), axis=0, tiled=True)]
    all_to_all x0 -> x1, starting transfers between devices: none -> 7.33 us  [local(): lax.all_to_all(jnp.broadcast_to(own_wanted, (devices, 1, own_wanted.shape...]
    reduce_min x0 -> x8, other arithmetic: none -> 7.12 us  [the longest x7 6.18 us: distinct_categories(): jnp.min(jnp.where(cand_cat > current[:, None], cand_cat, beyond), axis=1)]
    all_to_all x1, waiting for transfers between devices: 0.88 us -> 4.7 us  [local(): lax.all_to_all(pair_counts.astype(jnp.bfloat16), ('role', 'shard'), split...]
    all_to_all x0 -> x1, waiting for transfers between devices: none -> 3.56 us  [local(): lax.all_to_all(jnp.broadcast_to(own_wanted, (devices, 1, own_wanted.shape...]
    all_to_all x1, starting transfers between devices: 4.97 us -> 2.59 us  [local(): lax.all_to_all(packed, ('role', 'shard'), split_axis=0, concat_axis=1, ti...]
    reduce_or x1, other arithmetic: 1.54 us -> 0.07 us  [local(): hits = jnp.any(event_cat[:, :, None] == wanted[:, None, :], axis=-1)]
  transfers between devices with their start and end apart: 2 -> 3, of which waited for: 2 -> 3; matrix products, arithmetic and copies ran while one was open for 6% -> 10% of each run, Pallas kernels for 0% -> 0%
where the time goes in v1:
time: 66.9 us; the launch traced here: 66.1 us
  matrix products  20.5 us (31%)
  waiting for transfers between devices  18.9 us (28%)
  starting transfers between devices  12.4 us (19%)
  other arithmetic  8.15 us (12%)
  local copies, waits for them, and re-layouts  5.91 us (9%)
    all_to_all x1, waiting for transfers between devices, local(): lax.all_to_all(packed, ('role', 'shard'), split_axis=0, concat_axis=1, ti...  10.6 us
    all_to_all x1, starting transfers between devices, local(): lax.all_to_all(jnp.broadcast_to(own_wanted, (devices, 1, own_wanted.shape...  7.33 us
    reduce_min x7, other arithmetic, distinct_categories(): jnp.min(jnp.where(cand_cat > current[:, None], cand_cat, beyond), axis=1)  6.18 us
    sub x2, matrix products, attend(): expo = jnp.exp(scores - row_max)  5.72 us
    dot_general x2, matrix products, attend(): jnp.einsum('ghcs,gshk->gchk', weights, key_heads, preferred_element_type=...  5.23 us
    all_to_all x1, waiting for transfers between devices, local(): lax.all_to_all(pair_counts.astype(jnp.bfloat16), ('role', 'shard'), split...  4.7 us
    dot_general x1, matrix products, local(): jnp.dot(hidden, w_output, preferred_element_type=jnp.float32)  4.21 us
    all_to_all x1, waiting for transfers between devices, local(): lax.all_to_all(jnp.broadcast_to(own_wanted, (devices, 1, own_wanted.shape...  3.56 us
  transfers between devices with their start and end apart: 3, of which 3 were waited for; matrix products, arithmetic and copies ran while one was open for 10% of the time, Pallas kernels for 0%

profile of v1, /device:TPU:0, one launch (start us, length us, event | category | flops | bytes accessed | tf_op | source)
XLA Modules:
  0.0 66.1 jit_solution(547917875304710931)
XLA Ops:
  0.0 0.0 copy-start
  0.0 0.0 copy-start.1
  0.0 0.0 copy-start.3
  0.0 0.9 %reduce_min.86 = s32[8]{0:T(128)S(1)} reduce(s32[8,200]{1,0:T(8,128)} %param.11, s32[]{:T(128)} %constant.11.clone.1), dimensions={1}, to_apply=%region_0.0 | reduce | flops 1592 | bytes 6436 | tf_op jit(solution)/shard_map/reduce_min | solution.py:15
  0.9 0.9 %fusion.25 = s32[8]{0:T(128)S(1)} fusion(s32[8,200]{1,0:T(8,128)} %param.11, s32[8]{0:T(128)S(1)} %reduce_min.86), kind=kLoop, calls=%fused_computation.45 | loop fusion | flops 4792 | bytes 6464 | tf_op jit(solution)/shard_map/reduce_min | solution.py:18
  1.8 0.9 %fusion.26 = s32[8]{0:T(128)S(1)} fusion(s32[8,200]{1,0:T(8,128)} %param.11, s32[8]{0:T(128)S(1)} %compare_select_fusion.18), kind=kLoop, calls=%fused_computation.46 | loop fusion | flops 4792 | bytes 6464 | tf_op jit(solution)/shard_map/reduce_min | solution.py:18
  2.7 0.9 %fusion.27 = s32[8]{0:T(128)S(1)} fusion(s32[8,200]{1,0:T(8,128)} %param.11, s32[8]{0:T(128)S(1)} %compare_select_fusion.16), kind=kLoop, calls=%fused_computation.47 | loop fusion | flops 4792 | bytes 6464 | tf_op jit(solution)/shard_map/reduce_min | solution.py:18
  3.6 0.9 %fusion.28 = s32[8]{0:T(128)S(1)} fusion(s32[8,200]{1,0:T(8,128)} %param.11, s32[8]{0:T(128)S(1)} %compare_select_fusion.14), kind=kLoop, calls=%fused_computation.48 | loop fusion | flops 4792 | bytes 6464 | tf_op jit(solution)/shard_map/reduce_min | solution.py:18
  4.5 0.9 %fusion.29 = s32[8]{0:T(128)S(1)} fusion(s32[8,200]{1,0:T(8,128)} %param.11, s32[8]{0:T(128)S(1)} %compare_select_fusion.12), kind=kLoop, calls=%fused_computation.49 | loop fusion | flops 4792 | bytes 6464 | tf_op jit(solution)/shard_map/reduce_min | solution.py:18
  5.4 0.9 %fusion.30 = s32[8]{0:T(128)S(1)} fusion(s32[8,200]{1,0:T(8,128)} %param.11, s32[8]{0:T(128)S(1)} %compare_select_fusion.10), kind=kLoop, calls=%fused_computation.50 | loop fusion | flops 4792 | bytes 6464 | tf_op jit(solution)/shard_map/reduce_min | solution.py:18
  6.3 0.9 %fusion.31 = s32[8]{0:T(128)S(1)} fusion(s32[8,200]{1,0:T(8,128)} %param.11, s32[8]{0:T(128)S(1)} %compare_select_fusion.8), kind=kLoop, calls=%fused_computation.51 | loop fusion | flops 4792 | bytes 6464 | tf_op jit(solution)/shard_map/reduce_min | solution.py:18
  7.2 0.1 copy.37
  7.3 0.1 broadcast_in_dim.58
  7.4 0.6 broadcast_in_dim.59
  8.0 7.3 %all-to-all-start = ((s32[32,1,64]{2,1,0:T(1,128)}), s32[32,1,64]{2,1,0:T(1,128)S(1)}, u32[]{:S(2)}, u32[]{:S(2)}) async-start(s32[32,1,64]{2,1,0:T(1,128)} %broadcast_in_dim.59), calls=%async_computation | async-start | bytes 32768 | tf_op jit(solution)/shard_map/all_to_all | solution.py:46
  15.3 3.3 %fusion.23 = f32[1600,512]{1,0:T(8,128)} fusion(bf16[1600,128]{1,0:T(8,128)(2,1)} %bitcast.78, bf16[256,512]{1,0:T(8,128)(2,1)} %param.12), kind=kOutput, calls=%fused_computation.30 | convolution fusion | flops 209715200 | bytes 3817472 | tf_op jit(solution)/shard_map/dot_general | solution.py:61
  18.6 0.0 copy-done.1
  18.6 0.2 copy.48
  18.9 3.6 %all-to-all-done = s32[32,1,64]{2,1,0:T(1,128)S(1)} async-done(((s32[32,1,64]{2,1,0:T(1,128)}), s32[32,1,64]{2,1,0:T(1,128)S(1)}, u32[]{:S(2)}, u32[]{:S(2)}) %all-to-all-start) | async-done | bytes 8224 | tf_op jit(solution)/shard_map/all_to_all | solution.py:46
  22.4 0.5 broadcast.252
  22.9 0.7 %reduce.3 = s32[32,64]{1,0:T(8,128)S(1)} reduce(s32[32,1,64]{2,1,0:T(1,128)S(1)} %all-to-all-done, s32[]{:T(128)} %broadcast.252), dimensions={1}, to_apply=%all_to_all.24.reduce_sub_computation.3 | reduce | bytes 16388 | tf_op jit(solution)/shard_map/all_to_all | solution.py:46
  23.6 0.1 eq.229
  23.7 0.1 copy.38
  23.8 0.0 copy-done.3
  23.8 0.1 compare_reduce_fusion
  23.9 0.1 reshape.279
  24.1 0.1 copy.39
  24.2 0.2 convert_element_type.66
  24.3 0.9 %copy.44 = bf16[32,4,2]{1,2,0:T(2,128)(2,1)} copy(bf16[32,4,2]{2,1,0:T(4,128)(2,1)S(1)} %convert_element_type.66) | data formatting | bytes 1024 | tf_op jit(solution)/shard_map/convert_element_type | solution.py:76
  25.3 2.5 %all-to-all-start.2 = ((bf16[32,4,2]{1,2,0:T(2,128)(2,1)}), bf16[32,4,2]{1,2,0:T(2,128)(2,1)S(1)}, u32[]{:S(2)}, u32[]{:S(2)}) async-start(bf16[32,4,2]{1,2,0:T(2,128)(2,1)} %copy.44), calls=%async_computation.2 | async-start | bytes 32768 | tf_op jit(solution)/shard_map/all_to_all | solution.py:75
  27.8 0.1 stack.10
  27.8 0.1 add.34
  28.0 0.1 copy.40
  28.2 0.0 copy-done
  28.2 2.0 %bitcast_reduce_fusion = bf16[128,8,128]{2,1,0:T(8,128)(2,1)} fusion(bf16[256,20,128]{2,0,1:T(8,128)(2,1)S(1)} %copy-done, s32[256,20]{1,0:T(8,128)S(1)} %copy.40, pred[256,20]{1,0:T(8,128)(4,1)S(1)} %copy.39), kind=kOutput, calls=%fused_computation.22 | convolution fusion | flops 10698752 | bytes 1598464 | tf_op jit(solution)/shard_map/use,ued->usd/dot_general | solution.py:71
  30.2 4.7 %all-to-all-done.2 = bf16[32,4,2]{1,2,0:T(2,128)(2,1)S(1)} async-done(((bf16[32,4,2]{1,2,0:T(2,128)(2,1)}), bf16[32,4,2]{1,2,0:T(2,128)(2,1)S(1)}, u32[]{:S(2)}, u32[]{:S(2)}) %all-to-all-start.2) | async-done | bytes 544 | tf_op jit(solution)/shard_map/all_to_all | solution.py:75
  34.9 2.6 %all-to-all-start.1 = ((bf16[128,8,128]{2,1,0:T(8,128)(2,1)}), bf16[128,8,128]{2,1,0:T(8,128)(2,1)S(1)}, u32[]{:S(2)}, u32[]{:S(2)}) async-start(bf16[128,8,128]{2,1,0:T(8,128)(2,1)} %bitcast_reduce_fusion), calls=%async_computation.1 | async-start | bytes 524288 | tf_op jit(solution)/shard_map/all_to_all | solution.py:74
  37.6 0.1 copy.45
  37.6 0.1 copy.46
  37.7 0.1 broadcast_compare_fusion
  37.8 0.1 copy.47
  37.9 0.1 reshape_reshape.7
  38.1 10.6 %all-to-all-done.1 = bf16[128,8,128]{2,1,0:T(8,128)(2,1)S(1)} async-done(((bf16[128,8,128]{2,1,0:T(8,128)(2,1)}), bf16[128,8,128]{2,1,0:T(8,128)(2,1)S(1)}, u32[]{:S(2)}, u32[]{:S(2)}) %all-to-all-start.1) | async-done | bytes 262176 | tf_op jit(solution)/shard_map/all_to_all | solution.py:74
  48.7 0.1 copy.43
  48.9 0.0 copy-start.2
  48.9 0.0 copy-start.4
  49.0 12.9 %while.10 = (s32[]{:T(128)}, bf16[2,4,200,128]{3,2,1,0:T(8,128)(2,1)}, bf16[2,4,256,128]{2,3,1,0:T(8,128)(2,1)S(1)}, pred[2,4,256]{2,1,0:T(4,128)(4,1)S(1)}, bf16[2,4,200,128]{2,3,1,0:T(8,128)(2,1)S(1)}, /*index=5*/s32[]{:T(128)}) while((s32[]{:T(128)}, bf16[2,4,200,128]{3,2,1,0:T(8,128)(2,1)}, bf16[2,4,256,128]{2,3,1,0:T(8,128)(2,1)S(1)}, ...), condition=%wide.region_15.16_spmd, body=%wide.region_12.15_spmd.sunk | while | flops 109875456 | bytes 9269841 | solution.py:99
  49.1 2.9 %fusion.51 = (f32[4,4,200]{2,1,0:T(4,128)S(1)}, f32[4,4,200,256]{3,2,1,0:T(8,128)}) fusion(pred[4,256]{1,0:T(4,128)(4,1)S(1)} %dynamic-slice_bitcast_fusion.2, bf16[4,200,4,32]{1,3,2,0:T(8,128)(2,1)S(1)} %bitcast.74, bf16[4,256,4,32]{1,3,2,0:T(8,128)(2,1)S(1)} %bitcast.72), kind=kOutput, calls=%fused_computation.68.clone.1 | convolution fusion | flops 55705856 | bytes 3757568 | tf_op jit(solution)/shard_map/while/body/eval_jaxpr/sub | solution.py:36
  51.9 2.6 %fusion.52 = bf16[4,4,32,200]{3,2,1,0:T(8,128)(2,1)S(1)} fusion(bf16[4,256,4,32]{1,3,2,0:T(8,128)(2,1)S(1)} %bitcast.73, f32[4,4,200,256]{3,2,1,0:T(8,128)} %get-tuple-element.89, f32[4,4,200]{2,1,0:T(4,128)S(1)} %get-tuple-element.90), kind=kOutput, calls=%fused_computation.9.clone.1 | convolution fusion | flops 54169600 | bytes 3756544 | tf_op jit(solution)/shard_map/while/body/eval_jaxpr/ghcs,gshk->gchk/dot_general | solution.py:39
  54.5 0.2 copy.59
  54.7 0.7 %constant_dynamic-update-slice_fusion.2 = bf16[2,4,200,128]{3,2,1,0:T(8,128)(2,1)} fusion(bf16[2,4,200,128]{3,2,1,0:T(8,128)(2,1)} %get-tuple-element.98, bf16[1,4,200,128]{3,2,1,0:T(8,128)(2,1)S(1)} %copy.59, s32[]{:T(128)} %get-tuple-element.97), kind=kLoop, calls=%fused_computation.12.clone.1 | loop fusion | bytes 410112 | tf_op jit(solution)/shard_map/while/body/jit(dynamic_update_index_in_dim)/dynamic_update_slice | solution.py:99
  55.5 2.9 %fusion.51 = (f32[4,4,200]{2,1,0:T(4,128)S(1)}, f32[4,4,200,256]{3,2,1,0:T(8,128)}) fusion(pred[4,256]{1,0:T(4,128)(4,1)S(1)} %dynamic-slice_bitcast_fusion.2, bf16[4,200,4,32]{1,3,2,0:T(8,128)(2,1)S(1)} %bitcast.74, bf16[4,256,4,32]{1,3,2,0:T(8,128)(2,1)S(1)} %bitcast.72), kind=kOutput, calls=%fused_computation.68.clone.1 | convolution fusion | flops 55705856 | bytes 3757568 | tf_op jit(solution)/shard_map/while/body/eval_jaxpr/sub | solution.py:36
  58.4 2.6 %fusion.52 = bf16[4,4,32,200]{3,2,1,0:T(8,128)(2,1)S(1)} fusion(bf16[4,256,4,32]{1,3,2,0:T(8,128)(2,1)S(1)} %bitcast.73, f32[4,4,200,256]{3,2,1,0:T(8,128)} %get-tuple-element.89, f32[4,4,200]{2,1,0:T(4,128)S(1)} %get-tuple-element.90), kind=kOutput, calls=%fused_computation.9.clone.1 | convolution fusion | flops 54169600 | bytes 3756544 | tf_op jit(solution)/shard_map/while/body/eval_jaxpr/ghcs,gshk->gchk/dot_general | solution.py:39
  61.0 0.2 copy.59
  61.2 0.7 %constant_dynamic-update-slice_fusion.2 = bf16[2,4,200,128]{3,2,1,0:T(8,128)(2,1)} fusion(bf16[2,4,200,128]{3,2,1,0:T(8,128)(2,1)} %get-tuple-element.98, bf16[1,4,200,128]{3,2,1,0:T(8,128)(2,1)S(1)} %copy.59, s32[]{:T(128)} %get-tuple-element.97), kind=kLoop, calls=%fused_computation.12.clone.1 | loop fusion | bytes 410112 | tf_op jit(solution)/shard_map/while/body/jit(dynamic_update_index_in_dim)/dynamic_update_slice | solution.py:99
  61.9 0.0 copy-done.2
  61.9 0.0 copy-done.4
  61.9 4.2 %convolution_convert_fusion = bf16[1600,128]{1,0:T(8,128)(2,1)} fusion(bf16[512,128]{1,0:T(8,128)(2,1)S(1)} %copy-done.4, f32[1600,512]{1,0:T(8,128)} %fusion.23, bf16[1600,128]{1,0:T(8,128)(2,1)} %bitcast.85, bf16[256,512]{1,0:T(8,128)(2,1)S(1)} %copy-done.2), kind=kOutput, calls=%fused_computation.19 | convolution fusion | flops 424550400 | bytes 4358144 | tf_op jit(solution)/shard_map/dot_general | solution.py:110
  (26 shorter events, 0.4 us)
Async XLA Ops:
  0.0 28.2 %copy-start = (bf16[256,20,128]{2,0,1:T(8,128)(2,1)S(1)}, bf16[256,20,128]{2,0,1:T(8,128)(2,1)}, u32[]{:S(2)}) copy-start(bf16[256,20,128]{2,0,1:T(8,128)(2,1)} %param.8) | copy-start | bytes 3932164
  0.0 18.6 %copy-start.1 = (bf16[8,200,128]{2,1,0:T(8,128)(2,1)S(1)}, bf16[8,200,128]{2,1,0:T(8,128)(2,1)}, u32[]{:S(2)}) copy-start(bf16[8,200,128]{2,1,0:T(8,128)(2,1)} %param.10) | copy-start | bytes 1228804
  0.0 23.8 %copy-start.3 = (s32[256,20]{0,1:T(8,128)S(1)}, s32[256,20]{0,1:T(8,128)}, u32[]{:S(2)}) copy-start(s32[256,20]{0,1:T(8,128)} %param.9) | copy-start | bytes 61444
  8.0 14.4 %all-to-all-start = ((s32[32,1,64]{2,1,0:T(1,128)}), s32[32,1,64]{2,1,0:T(1,128)S(1)}, u32[]{:S(2)}, u32[]{:S(2)}) async-start(s32[32,1,64]{2,1,0:T(1,128)} %broadcast_in_dim.59), calls=%async_computation | async-start | bytes 32768 | tf_op jit(solution)/shard_map/all_to_all | solution.py:46
  25.3 9.6 %all-to-all-start.2 = ((bf16[32,4,2]{1,2,0:T(2,128)(2,1)}), bf16[32,4,2]{1,2,0:T(2,128)(2,1)S(1)}, u32[]{:S(2)}, u32[]{:S(2)}) async-start(bf16[32,4,2]{1,2,0:T(2,128)(2,1)} %copy.44), calls=%async_computation.2 | async-start | bytes 32768 | tf_op jit(solution)/shard_map/all_to_all | solution.py:75
  34.9 13.8 %all-to-all-start.1 = ((bf16[128,8,128]{2,1,0:T(8,128)(2,1)}), bf16[128,8,128]{2,1,0:T(8,128)(2,1)S(1)}, u32[]{:S(2)}, u32[]{:S(2)}) async-start(bf16[128,8,128]{2,1,0:T(8,128)(2,1)} %bitcast_reduce_fusion), calls=%async_computation.1 | async-start | bytes 524288 | tf_op jit(solution)/shard_map/all_to_all | solution.py:74
  48.9 12.9 %copy-start.2 = (bf16[256,512]{1,0:T(8,128)(2,1)S(1)}, bf16[256,512]{1,0:T(8,128)(2,1)}, u32[]{:S(2)}) copy-start(bf16[256,512]{1,0:T(8,128)(2,1)} %param.12) | copy-start | bytes 786436
  48.9 12.9 %copy-start.4 = (bf16[512,128]{1,0:T(8,128)(2,1)S(1)}, bf16[512,128]{1,0:T(8,128)(2,1)}, u32[]{:S(2)}) copy-start(bf16[512,128]{1,0:T(8,128)(2,1)} %param.13) | copy-start | bytes 393220

commit v2 on v0

v2 whole, which is shorter than its diff:
```python
import math

import jax
import jax.numpy as jnp
from jax import lax
from jax.experimental import pallas as pl
from jax.experimental.pallas import tpu as pltpu
from jax.sharding import PartitionSpec as P

HEADS = 4
CAP = 8
QCAT = 8
LANES = 128
FINE = 8
BARRED = -1e30
AXES = ("role", "shard")


def iota(shape, dimension):
    return lax.broadcasted_iota(jnp.int32, shape, dimension)


def distinct_kernel(cat_ref, out_ref):
    cats = cat_ref[...].astype(jnp.float32)
    users = cats.shape[0]
    half = LANES // 2
    user = iota((users, LANES), 0)
    lane = iota((users, LANES), 1)
    beyond = jnp.float32(1e9)
    low = jnp.min(cats, axis=1, keepdims=True)
    high = jnp.max(cats, axis=1, keepdims=True)
    row = jnp.zeros((users, LANES), jnp.float32)
    for step in range(QCAT // 2):
        for place, value in ((step, low), (QCAT - 1 - step, high)):
            row = jnp.where(lane % half == place * users + user, value, row)
        if step + 1 < QCAT // 2:
            above = jnp.min(jnp.where(cats > low, cats, beyond), axis=1, keepdims=True)
            below = jnp.max(jnp.where(cats < high, cats, -beyond), axis=1, keepdims=True)
            low = jnp.where(above == beyond, low, above)
            high = jnp.where(below == -beyond, high, below)
    whole = jnp.sum(row, axis=0, keepdims=True).astype(jnp.int32)
    fine = whole & (FINE - 1)
    packed = jnp.where(iota((1, LANES), 1) < half, whole - fine, fine)
    out_ref[...] = jnp.broadcast_to(packed.reshape(1, 1, LANES), out_ref.shape)


def pack_kernel(wanted_ref, event_ref, history_ref, out_ref, *, own_users):
    devices = wanted_ref.shape[0]
    blocks_events = history_ref.shape[0]
    width = history_ref.shape[2]
    depth = event_ref.shape[1]
    span = depth // blocks_events
    per_group = span // own_users
    pairs = own_users // 2
    half = LANES // 2
    pad = -(-depth // LANES) * LANES
    wanted = wanted_ref[:, 0, :].astype(jnp.float32).astype(jnp.bfloat16)
    line = iota((LANES, pad), 0) % half
    mate = iota((LANES, pad), 1) % own_users
    events = event_ref[...].astype(jnp.float32)
    match = None
    for j in range(QCAT):
        spread = jnp.where(line == j * own_users + mate, 1.0, 0.0).astype(jnp.bfloat16)
        category = jnp.dot(wanted, spread, preferred_element_type=jnp.float32)[:, :depth]
        same = jnp.where(category == events, 1.0, 0.0)
        match = same if match is None else jnp.maximum(match, same)
    position = iota((devices, depth), 1) % span
    mine = position // own_users == iota((devices, depth), 0) % per_group
    match = jnp.where(mine, match, 0.0)
    before = iota((depth, pad), 0)
    here = iota((depth, pad), 1)
    user_before = before % span
    user_here = here % span
    counted = (user_before == user_here) & (before <= here)
    counted = counted | ((user_here % 2 == 1) & (user_before == user_here - 1))
    counted = jnp.where(counted, 1.0, 0.0).astype(jnp.bfloat16)
    matched = match.astype(jnp.bfloat16)
    place = jnp.dot(matched, counted, preferred_element_type=jnp.float32)[:, :depth]
    pair_base = ((position % own_users) // 2 * CAP - 1).astype(jnp.float32)
    code = jnp.where(match > 0.0, place + pair_base, -1.0)
    lane = iota((depth, LANES), 1)
    leading = (lane < 2 * pairs) & (iota((depth, LANES), 0) % own_users == 2 * (lane % pairs))
    leading = jnp.where(leading, 1.0, 0.0).astype(jnp.bfloat16)
    lead = jnp.dot(matched, leading, preferred_element_type=jnp.float32)
    rows = pairs * CAP
    row = iota((rows, depth), 0).astype(jnp.float32)
    rank = iota((CAP, LANES), 0).astype(jnp.float32)
    first = iota((CAP, LANES), 1) < pairs
    for group in range(devices // per_group):
        stored = history_ref[:, group * span : (group + 1) * span, :].reshape(depth, width)
        picks = []
        for member in range(per_group):
            device = group * per_group + member
            picks.append(jnp.where(row == code[device : device + 1, :], 1.0, 0.0).astype(jnp.bfloat16))
        packed = jnp.dot(jnp.concatenate(picks, axis=0), stored, preferred_element_type=jnp.float32)
        packed = packed.astype(jnp.bfloat16)
        for member in range(per_group):
            device = group * per_group + member
            out_ref[device, :rows, :] = packed[member * rows : (member + 1) * rows, :]
            is_lead = rank < lead[device : device + 1, :]
            barred = jnp.where(is_lead == first, 0.0, BARRED)
            out_ref[device, rows:, :] = barred.astype(jnp.bfloat16)


def tower_kernel(key_ref, bar_ref, cand_ref, w_in_ref, w_out_ref, out_ref, *, pairs):
    pair = pl.program_id(0)
    rows, width = cand_ref.shape
    slots = key_ref.shape[0] * CAP
    head_size = width // HEADS
    scale = math.log2(math.e) * head_size ** (-0.5)
    cands = cand_ref[...]
    keys = key_ref[...].reshape(slots, width)
    lane_row = iota((rows, LANES), 1)
    second = jnp.where(iota((rows, LANES), 0) >= rows // 2, pairs, 0)
    chosen = jnp.where(lane_row == pair + second, 1.0, 0.0).astype(jnp.bfloat16)
    right = jnp.concatenate([keys, bar_ref[...].reshape(slots, LANES)], axis=1)
    values = jnp.concatenate([keys, jnp.ones((slots, width), jnp.bfloat16)], axis=1)
    head_of = iota((rows, width), 1) // head_size
    interest = jnp.zeros((rows, width), jnp.float32)
    total = jnp.zeros((rows, width), jnp.float32)
    for head in range(HEADS):
        queries = jnp.where(head_of == head, cands.astype(jnp.float32), 0.0).astype(jnp.bfloat16)
        left = jnp.concatenate([queries, chosen], axis=1)
        scores = lax.dot_general(left, right, (((1,), (1,)), ((), ())), preferred_element_type=jnp.float32)
        peak = jnp.max(scores, axis=1, keepdims=True)
        expo = jnp.exp2((scores - peak) * scale).astype(jnp.bfloat16)
        both = jnp.dot(expo, values, preferred_element_type=jnp.float32)
        interest = jnp.where(head_of == head, both[:, :width], interest)
        total = jnp.where(head_of == head, both[:, width:], total)
    interest = (interest / total).astype(jnp.bfloat16)
    hidden = jnp.dot(
        jnp.concatenate([cands, interest], axis=1), w_in_ref[...], preferred_element_type=jnp.float32
    )
    middle = hidden * 0.5
    hidden = (middle * jnp.tanh(middle) + middle).astype(jnp.bfloat16)
    result = jnp.dot(hidden, w_out_ref[...], preferred_element_type=jnp.float32)
    out_ref[...] = result.astype(jnp.bfloat16)


def exchange(parts):
    return lax.all_to_all(parts, AXES, split_axis=0, concat_axis=0, tiled=True)


def local(history, event_cat, candidates, cand_cat, w_input, w_output):
    devices = lax.axis_size(AXES)
    own_users, cand_count, width = candidates.shape
    users, block_events = event_cat.shape
    pairs = own_users // 2
    wanted = pl.pallas_call(
        distinct_kernel,
        out_shape=jax.ShapeDtypeStruct((devices, 1, LANES), jnp.int32),
        name="distinct",
    )(cand_cat)
    wanted = exchange(wanted)
    span = math.lcm(16, own_users)
    grouped = event_cat.T.reshape(block_events, users // span, span).transpose(1, 0, 2)
    grouped = jnp.repeat(grouped.reshape(users // span, block_events * span), span // own_users, axis=0)
    packed = pl.pallas_call(
        lambda *refs: pack_kernel(*refs, own_users=own_users),
        out_shape=jax.ShapeDtypeStruct((devices, (pairs + 1) * CAP, width), jnp.bfloat16),
        name="pack",
    )(wanted, grouped, history.transpose(1, 0, 2))
    received = exchange(packed)
    rows = own_users * cand_count
    result = pl.pallas_call(
        lambda *refs: tower_kernel(*refs, pairs=pairs),
        out_shape=jax.ShapeDtypeStruct((rows, width), jnp.bfloat16),
        grid=(pairs,),
        in_specs=[
            pl.BlockSpec((devices, CAP, width), lambda i: (0, i, 0)),
            pl.BlockSpec((devices, CAP, width), lambda i: (0, pairs, 0)),
            pl.BlockSpec((rows // pairs, width), lambda i: (i, 0)),
            pl.BlockSpec(w_input.shape, lambda i: (0, 0)),
            pl.BlockSpec(w_output.shape, lambda i: (0, 0)),
        ],
        out_specs=pl.BlockSpec((rows // pairs, width), lambda i: (i, 0)),
        name="tower",
    )(received, received, candidates.reshape(rows, width), w_input, w_output)
    return result.reshape(own_users, cand_count, width)


def solution(mesh):
    placed = (
        P(None, AXES, None),
        P(None, AXES),
        P(AXES, None, None),
        P(AXES, None),
        P(),
        P(),
    )
    return jax.shard_map(
        local,
        mesh=mesh,
        in_specs=placed,
        out_specs=P(AXES, None, None),
        check_vma=False,
    )
```

time: 118 us -> 43 us (0.36)
  blocking collectives: 71.8 us -> 15.9 us
  matrix products: 20.5 us -> 0 us
  Pallas kernels: 0 us -> 11.8 us
  waiting for transfers between devices: 11.5 us -> 5.39 us
  local copies, waits for them, and re-layouts: 4.56 us -> 2.26 us
  other arithmetic: 1.77 us -> 0 us
    all_gather x1 -> x0, blocking collectives: 71.8 us -> none  [local(): wanted = lax.all_gather(cand_cat, ('role', 'shard'), axis=0, tiled=True)]
    all_to_all x0 -> x1, blocking collectives: none -> 15.9 us  [exchange(): return lax.all_to_all(parts, AXES, split_axis=0, concat_axis=0, tiled=True)]
    dot_general x5 -> x0, matrix products: 14.8 us -> none  [the longest x2 5.23 us: attend(): jnp.einsum('ghcs,gshk->gchk', weights, key_heads, preferred_element_type=...]
    pallas_call x0 -> x3, Pallas kernels: none -> 11.8 us  [the longest x1 7.25 us: local(): pl.pallas_call(lambda *refs: tower_kernel(*refs, pairs=pairs), out_shape=...]
    all_to_all x2 -> x1, waiting for transfers between devices: 11.5 us -> 5.39 us  [exchange(): return lax.all_to_all(parts, AXES, split_axis=0, concat_axis=0, tiled=True)]
    sub x2 -> x0, matrix products: 5.73 us -> none  [attend(): expo = jnp.exp(scores - row_max)]
    dynamic_update_slice x4 -> x0, local copies, waits for them, and re-layouts: 1.78 us -> none  [local(): lax.map(one_pack, (candidates.reshape(packs, group, cand_count, width), r...]
    reduce_or x1 -> x0, other arithmetic: 1.54 us -> none  [local(): hits = jnp.any(event_cat[:, :, None] == wanted[:, None, :], axis=-1)]
  transfers between devices with their start and end apart: 2 -> 1, of which waited for: 2 -> 1; matrix products, arithmetic and copies ran while one was open for 6% -> 4% of each run, Pallas kernels for 0% -> 0%
where the time goes in v2:
time: 43 us; the launch traced here: 42.7 us
  blocking collectives  15.9 us (37%)
  Pallas kernels  11.8 us (27%)
  starting transfers between devices  7.33 us (17%)
  waiting for transfers between devices  5.39 us (13%)
  local copies, waits for them, and re-layouts  2.26 us (5%)
    all_to_all x1, blocking collectives, exchange(): return lax.all_to_all(parts, AXES, split_axis=0, concat_axis=0, tiled=True)  15.9 us
    all_to_all x1, starting transfers between devices, exchange(): return lax.all_to_all(parts, AXES, split_axis=0, concat_axis=0, tiled=True)  7.33 us
    pallas_call x1, Pallas kernels, local(): pl.pallas_call(lambda *refs: tower_kernel(*refs, pairs=pairs), out_shape=...  7.25 us
    all_to_all x1, waiting for transfers between devices, exchange(): return lax.all_to_all(parts, AXES, split_axis=0, concat_axis=0, tiled=True)  5.39 us
    pallas_call x1, Pallas kernels, local(): pl.pallas_call(lambda *refs: pack_kernel(*refs, own_users=own_users), out...  2.91 us
    pallas_call x1, Pallas kernels, local(): pl.pallas_call(distinct_kernel, out_shape=jax.ShapeDtypeStruct((devices,...  1.64 us
  transfers between devices with their start and end apart: 1, of which 1 were waited for; matrix products, arithmetic and copies ran while one was open for 4% of the time, Pallas kernels for 0%

profile of v2, /device:TPU:0, one launch (start us, length us, event | category | flops | bytes accessed | tf_op | source)
XLA Modules:
  0.0 42.7 jit_solution(9631213509707063254)
XLA Ops:
  0.0 1.6 %distinct.1 = s32[32,1,128]{2,1,0:T(1,128)} custom-call(s32[8,200]{1,0:T(8,128)} %cat_ref.1), custom_call_target="tpu_custom_call" | custom-call | tf_op jit(solution)/shard_map/distinct/pallas_call | solution.py:149
  1.6 7.3 %all-to-all-start = ((s32[32,1,128]{2,1,0:T(1,128)}), s32[32,1,128]{2,1,0:T(1,128)S(1)}, u32[]{:S(2)}, u32[]{:S(2)}) async-start(s32[32,1,128]{2,1,0:T(1,128)} %distinct.1), calls=%async_computation | async-start | bytes 32768 | tf_op jit(solution)/shard_map/all_to_all | solution.py:141
  9.0 0.8 %reshape.15 = s32[20,16,16]{2,1,0:T(8,128)S(1)} reshape(s32[20,256]{1,0:T(8,128)} %bitcast.8) | data formatting | bytes 40960 | tf_op jit(solution)/shard_map/reshape | solution.py:156
  9.8 0.1 copy.7
  9.9 0.1 reshape.16
  10.0 0.6 %reshape.17.refs_1_ = s32[32,320]{1,0:T(8,128)} reshape(s32[16,2,320]{2,1,0:T(2,128)S(1)} %broadcast_in_dim.3) | data formatting | bytes 81920 | tf_op jit(solution)/shard_map/reshape | solution.py:157
  10.7 5.4 %all-to-all-done.refs_0_ = s32[32,1,128]{2,1,0:T(1,128)S(1)} async-done(((s32[32,1,128]{2,1,0:T(1,128)}), s32[32,1,128]{2,1,0:T(1,128)S(1)}, u32[]{:S(2)}, u32[]{:S(2)}) %all-to-all-start) | async-done | bytes 16416 | tf_op jit(solution)/shard_map/all_to_all | solution.py:141
  16.1 0.0 copy-start
  16.1 0.6 %copy-done = s32[32,1,128]{2,1,0:T(1,128)} copy-done((s32[32,1,128]{2,1,0:T(1,128)}, s32[32,1,128]{2,1,0:T(1,128)S(1)}, u32[]{:S(2)}) %copy-start) | copy-done | bytes 16408
  16.6 2.9 %pack.1 = bf16[32,40,128]{2,1,0:T(8,128)(2,1)} custom-call(s32[32,1,128]{2,1,0:T(1,128)} %copy-done, s32[32,320]{1,0:T(8,128)} %reshape.17.refs_1_, bf16[20,256,128]{2,1,0:T(8,128)(2,1)} %bitcast.5), custom_call_target="tpu_custom_call" | custom-call | tf_op jit(solution)/shard_map/pack/pallas_call | solution.py:158
  19.6 15.9 %all_to_all.10.refs_0_.refs_1_ = bf16[32,40,128]{2,1,0:T(8,128)(2,1)} all-to-all(bf16[32,40,128]{2,1,0:T(8,128)(2,1)} %pack.1), channel_id=1, replica_groups=mesh['role'=2,'shard'=16] {'role','shard'}, dimensions={0} | all-to-all | bytes 655360 | tf_op jit(solution)/shard_map/all_to_all | solution.py:141
  35.4 7.2 %tower.1 = bf16[1600,128]{1,0:T(8,128)(2,1)} custom-call(bf16[32,40,128]{2,1,0:T(8,128)(2,1)} %all_to_all.10.refs_0_.refs_1_, bf16[32,40,128]{2,1,0:T(8,128)(2,1)} %all_to_all.10.refs_0_.refs_1_, bf16[1600,128]{1,0:T(8,128)(2,1)} %bitcast.7, bf16[256,512]{1,0:T(8,128)(2,1)} %refs_3_.1, bf16[512,128]{1,0:T(8,128)(2,1)} %refs_4_.1), custom_call_target="tpu_custom_call" | custom-call | tf_op jit(solution)/shard_map/tower/pallas_call | solution.py:165
  (1 shorter events, 0.0 us)
Async XLA Ops:
  1.6 14.4 %all-to-all-start = ((s32[32,1,128]{2,1,0:T(1,128)}), s32[32,1,128]{2,1,0:T(1,128)S(1)}, u32[]{:S(2)}, u32[]{:S(2)}) async-start(s32[32,1,128]{2,1,0:T(1,128)} %distinct.1), calls=%async_computation | async-start | bytes 32768 | tf_op jit(solution)/shard_map/all_to_all | solution.py:141
  16.1 0.6 %copy-start = (s32[32,1,128]{2,1,0:T(1,128)}, s32[32,1,128]{2,1,0:T(1,128)S(1)}, u32[]{:S(2)}) copy-start(s32[32,1,128]{2,1,0:T(1,128)S(1)} %all-to-all-done.refs_0_) | copy-start | bytes 49156

commit v3 on v2

--- a/solution.py
+++ b/solution.py
@@ -13,6 +13,7 @@
 LANES = 128
 FINE = 8
 BARRED = -1e30
+MEBI = 1 << 20
 AXES = ("role", "shard")
 
 
@@ -79,13 +80,12 @@
     pair_base = ((position % own_users) // 2 * CAP - 1).astype(jnp.float32)
     code = jnp.where(match > 0.0, place + pair_base, -1.0)
     lane = iota((depth, LANES), 1)
-    leading = (lane < 2 * pairs) & (iota((depth, LANES), 0) % own_users == 2 * (lane % pairs))
+    leading = (lane < pairs) & (iota((depth, LANES), 0) % own_users == 2 * lane)
     leading = jnp.where(leading, 1.0, 0.0).astype(jnp.bfloat16)
     lead = jnp.dot(matched, leading, preferred_element_type=jnp.float32)
     rows = pairs * CAP
     row = iota((rows, depth), 0).astype(jnp.float32)
     rank = iota((CAP, LANES), 0).astype(jnp.float32)
-    first = iota((CAP, LANES), 1) < pairs
     for group in range(devices // per_group):
         stored = history_ref[:, group * span : (group + 1) * span, :].reshape(depth, width)
         picks = []
@@ -97,44 +97,70 @@
         for member in range(per_group):
             device = group * per_group + member
             out_ref[device, :rows, :] = packed[member * rows : (member + 1) * rows, :]
-            is_lead = rank < lead[device : device + 1, :]
-            barred = jnp.where(is_lead == first, 0.0, BARRED)
-            out_ref[device, rows:, :] = barred.astype(jnp.bfloat16)
-
-
-def tower_kernel(key_ref, bar_ref, cand_ref, w_in_ref, w_out_ref, out_ref, *, pairs):
-    pair = pl.program_id(0)
-    rows, width = cand_ref.shape
-    slots = key_ref.shape[0] * CAP
+            mark = jnp.where(rank < lead[device : device + 1, :], 1.0, 0.0)
+            out_ref[device, rows:, :] = mark.astype(jnp.bfloat16)
+
+
+def tower_kernel(packed_ref, cand_ref, w_in_ref, w_out_ref, out_ref):
+    own_users, cand_count, width = cand_ref.shape
+    pairs = own_users // 2
+    devices = packed_ref.shape[0]
+    slots = devices * CAP
     head_size = width // HEADS
     scale = math.log2(math.e) * head_size ** (-0.5)
-    cands = cand_ref[...]
-    keys = key_ref[...].reshape(slots, width)
-    lane_row = iota((rows, LANES), 1)
-    second = jnp.where(iota((rows, LANES), 0) >= rows // 2, pairs, 0)
-    chosen = jnp.where(lane_row == pair + second, 1.0, 0.0).astype(jnp.bfloat16)
-    right = jnp.concatenate([keys, bar_ref[...].reshape(slots, LANES)], axis=1)
-    values = jnp.concatenate([keys, jnp.ones((slots, width), jnp.bfloat16)], axis=1)
-    head_of = iota((rows, width), 1) // head_size
-    interest = jnp.zeros((rows, width), jnp.float32)
-    total = jnp.zeros((rows, width), jnp.float32)
-    for head in range(HEADS):
-        queries = jnp.where(head_of == head, cands.astype(jnp.float32), 0.0).astype(jnp.bfloat16)
-        left = jnp.concatenate([queries, chosen], axis=1)
-        scores = lax.dot_general(left, right, (((1,), (1,)), ((), ())), preferred_element_type=jnp.float32)
-        peak = jnp.max(scores, axis=1, keepdims=True)
-        expo = jnp.exp2((scores - peak) * scale).astype(jnp.bfloat16)
-        both = jnp.dot(expo, values, preferred_element_type=jnp.float32)
-        interest = jnp.where(head_of == head, both[:, :width], interest)
-        total = jnp.where(head_of == head, both[:, width:], total)
-    interest = (interest / total).astype(jnp.bfloat16)
-    hidden = jnp.dot(
-        jnp.concatenate([cands, interest], axis=1), w_in_ref[...], preferred_element_type=jnp.float32
-    )
-    middle = hidden * 0.5
-    hidden = (middle * jnp.tanh(middle) + middle).astype(jnp.bfloat16)
-    result = jnp.dot(hidden, w_out_ref[...], preferred_element_type=jnp.float32)
-    out_ref[...] = result.astype(jnp.bfloat16)
+    marks = packed_ref[:, pairs * CAP :, :].reshape(slots, LANES)
+    pick = jnp.where(iota((2 * CAP, LANES), 0) == iota((2 * CAP, LANES), 1), 1.0, 0.0).astype(jnp.bfloat16)
+    across = lax.dot_general(pick, marks, (((1,), (1,)), ((), ())), preferred_element_type=jnp.float32)
+    marks = marks.astype(jnp.float32)
+    slot_head = iota((slots, width), 1) // head_size
+    head_of = iota((cand_count, width), 1) // head_size
+    w_in = w_in_ref[...]
+    w_out = w_out_ref[...]
+    for pair in range(pairs):
+        keys = packed_ref[:, pair * CAP : (pair + 1) * CAP, :].reshape(slots, width).astype(jnp.float32)
+        owned = jnp.broadcast_to(marks[:, pair : pair + 1], (slots, width)) > 0.5
+        own_keys = (jnp.where(owned, keys, 0.0), jnp.where(owned, 0.0, keys))
+        ones = (jnp.where(owned, 1.0, 0.0), jnp.where(owned, 0.0, 1.0))
+        right = jnp.concatenate([part.astype(jnp.bfloat16) for part in own_keys], axis=1)
+        values = []
+        for parity in range(2):
+            mixed = [jnp.where(slot_head % 2 == parity, k, o).astype(jnp.bfloat16) for k, o in zip(own_keys, ones)]
+            values.append(jnp.concatenate(mixed, axis=1))
+        first = jnp.broadcast_to(across[pair : pair + 1, :], (cand_count, slots)) > 0.5
+        cands = [cand_ref[2 * pair + member].astype(jnp.float32) for member in range(2)]
+        tops = [jnp.zeros((cand_count, width), jnp.float32)] * 2
+        totals = [jnp.ones((cand_count, width), jnp.float32)] * 2
+        for head in range(HEADS):
+            left = jnp.concatenate(
+                [jnp.where(head_of == head, c, 0.0).astype(jnp.bfloat16) for c in cands], axis=1
+            )
+            scores = lax.dot_general(left, right, (((1,), (1,)), ((), ())), preferred_element_type=jnp.float32)
+            peak_first = jnp.max(jnp.where(first, scores, BARRED), axis=1, keepdims=True)
+            peak_second = jnp.max(jnp.where(first, BARRED, scores), axis=1, keepdims=True)
+            expo = jnp.exp2((scores - jnp.where(first, peak_first, peak_second)) * scale).astype(jnp.bfloat16)
+            both = jnp.dot(expo, values[head % 2], preferred_element_type=jnp.float32)
+            for member in range(2):
+                part = both[:, member * width : (member + 1) * width]
+                tops[member] = jnp.where(head_of == head, part, tops[member])
+                totals[member] = jnp.where(head_of == head ^ 1, part, totals[member])
+        for member in range(2):
+            inverse = 1.0 / totals[member]
+            inverse = jnp.where(
+                head_of % 2 == 0,
+                pltpu.roll(inverse, width - head_size, 1),
+                pltpu.roll(inverse, head_size, 1),
+            )
+            interest = (tops[member] * inverse).astype(jnp.bfloat16)
+            joined = jnp.concatenate([cand_ref[2 * pair + member], interest], axis=1)
+            hidden = jnp.dot(joined, w_in, preferred_element_type=jnp.float32)
+            middle = hidden * 0.5
+            hidden = (middle * jnp.tanh(middle) + middle).astype(jnp.bfloat16)
+            result = jnp.dot(hidden, w_out, preferred_element_type=jnp.float32)
+            out_ref[2 * pair + member] = result.astype(jnp.bfloat16)
+
+
+def near(value):
+    return pltpu.with_memory_space_constraint(value, pltpu.VMEM)
 
 
 def exchange(parts):
@@ -149,34 +175,29 @@
     wanted = pl.pallas_call(
         distinct_kernel,
         out_shape=jax.ShapeDtypeStruct((devices, 1, LANES), jnp.int32),
+        compiler_params=pltpu.CompilerParams(vmem_limit_bytes=4 * MEBI),
         name="distinct",
     )(cand_cat)
     wanted = exchange(wanted)
+    resident = pl.BlockSpec(memory_space=pltpu.VMEM)
     span = math.lcm(16, own_users)
     grouped = event_cat.T.reshape(block_events, users // span, span).transpose(1, 0, 2)
     grouped = jnp.repeat(grouped.reshape(users // span, block_events * span), span // own_users, axis=0)
     packed = pl.pallas_call(
         lambda *refs: pack_kernel(*refs, own_users=own_users),
         out_shape=jax.ShapeDtypeStruct((devices, (pairs + 1) * CAP, width), jnp.bfloat16),
+        in_specs=[resident] * 3,
+        compiler_params=pltpu.CompilerParams(vmem_limit_bytes=24 * MEBI),
         name="pack",
-    )(wanted, grouped, history.transpose(1, 0, 2))
+    )(near(wanted), near(grouped), near(history.transpose(1, 0, 2)))
     received = exchange(packed)
-    rows = own_users * cand_count
-    result = pl.pallas_call(
-        lambda *refs: tower_kernel(*refs, pairs=pairs),
-        out_shape=jax.ShapeDtypeStruct((rows, width), jnp.bfloat16),
-        grid=(pairs,),
-        in_specs=[
-            pl.BlockSpec((devices, CAP, width), lambda i: (0, i, 0)),
-            pl.BlockSpec((devices, CAP, width), lambda i: (0, pairs, 0)),
-            pl.BlockSpec((rows // pairs, width), lambda i: (i, 0)),
-            pl.BlockSpec(w_input.shape, lambda i: (0, 0)),
-            pl.BlockSpec(w_output.shape, lambda i: (0, 0)),
-        ],
-        out_specs=pl.BlockSpec((rows // pairs, width), lambda i: (i, 0)),
+    return pl.pallas_call(
+        tower_kernel,
+        out_shape=jax.ShapeDtypeStruct(candidates.shape, jnp.bfloat16),
+        in_specs=[resident] * 4,
+        compiler_params=pltpu.CompilerParams(vmem_limit_bytes=32 * MEBI),
         name="tower",
-    )(received, received, candidates.reshape(rows, width), w_input, w_output)
-    return result.reshape(own_users, cand_count, width)
+    )(near(received), near(candidates), near(w_input), near(w_output))
 
 
 def solution(mesh):

time: 43 us -> 40.7 us (0.947)
  Pallas kernels: 11.8 us -> 9.62 us
  blocking collectives: 15.9 us -> 14.3 us
  local copies, waits for them, and re-layouts: 2.26 us -> 3.08 us
  waiting for transfers between devices: 5.39 us -> 5.97 us
    pallas_call x1, Pallas kernels: 2.91 us -> 0.81 us  [local(): pl.pallas_call(lambda *refs: pack_kernel(*refs, own_users=own_users), out...]
    all_to_all x1, blocking collectives: 15.9 us -> 14.3 us  [exchange(): return lax.all_to_all(parts, AXES, split_axis=0, concat_axis=0, tiled=True)]
    unnamed x2 -> x10, local copies, waits for them, and re-layouts: 0.6 us -> 2.03 us
    pallas_call x1, Pallas kernels: 1.64 us -> 0.94 us  [local(): pl.pallas_call(distinct_kernel, out_shape=jax.ShapeDtypeStruct((devices,...]
    pallas_call x1, Pallas kernels: 7.25 us -> 7.87 us  [local(): pl.pallas_call(tower_kernel, out_shape=jax.ShapeDtypeStruct(candidates.sh...]
    reshape x1, local copies, waits for them, and re-layouts: 0.64 us -> 0.04 us  [local(): jnp.repeat(grouped.reshape(users // span, block_events * span), span // o...]
    all_to_all x1, waiting for transfers between devices: 5.39 us -> 5.97 us  [exchange(): return lax.all_to_all(parts, AXES, split_axis=0, concat_axis=0, tiled=True)]
  transfers between devices with their start and end apart: 1 -> 1, of which waited for: 1 -> 1; matrix products, arithmetic and copies ran while one was open for 4% -> 3% of each run, Pallas kernels for 0% -> 0%
where the time goes in v3:
time: 40.7 us; the launch traced here: 40.4 us
  blocking collectives  14.3 us (35%)
  Pallas kernels  9.62 us (24%)
  starting transfers between devices  7.33 us (18%)
  waiting for transfers between devices  5.97 us (15%)
  local copies, waits for them, and re-layouts  3.08 us (8%)
    all_to_all x1, blocking collectives, exchange(): return lax.all_to_all(parts, AXES, split_axis=0, concat_axis=0, tiled=True)  14.3 us
    pallas_call x1, Pallas kernels, local(): pl.pallas_call(tower_kernel, out_shape=jax.ShapeDtypeStruct(candidates.sh...  7.87 us
    all_to_all x1, starting transfers between devices, exchange(): return lax.all_to_all(parts, AXES, split_axis=0, concat_axis=0, tiled=True)  7.33 us
    all_to_all x1, waiting for transfers between devices, exchange(): return lax.all_to_all(parts, AXES, split_axis=0, concat_axis=0, tiled=True)  5.97 us
    unnamed x10, local copies, waits for them, and re-layouts  2.03 us
    pallas_call x1, Pallas kernels, local(): pl.pallas_call(distinct_kernel, out_shape=jax.ShapeDtypeStruct((devices,...  0.94 us
    reshape x1, local copies, waits for them, and re-layouts, local(): event_cat.T.reshape(block_events, users // span, span).transpose(1, 0, 2)  0.84 us
  transfers between devices with their start and end apart: 1, of which 1 were waited for; matrix products, arithmetic and copies ran while one was open for 3% of the time, Pallas kernels for 0%

profile of v3, /device:TPU:0, one launch (start us, length us, event | category | flops | bytes accessed | tf_op | source)
XLA Modules:
  0.0 40.4 jit_solution(4302518415446381788)
XLA Ops:
  0.0 0.0 copy-start.4
  0.0 0.7 %copy-done.4 = s32[8,200]{1,0:T(8,128)S(1)} copy-done((s32[8,200]{1,0:T(8,128)S(1)}, s32[8,200]{1,0:T(8,128)}, u32[]{:S(2)}) %copy-start.4) | copy-done | bytes 6424
  0.7 0.9 %distinct.1 = s32[32,1,128]{2,1,0:T(1,128)} custom-call(s32[8,200]{1,0:T(8,128)S(1)} %copy-done.4), custom_call_target="tpu_custom_call" | custom-call | tf_op jit(solution)/shard_map/distinct/pallas_call | solution.py:175
  1.6 7.3 %all-to-all-start = ((s32[32,1,128]{2,1,0:T(1,128)}), s32[32,1,128]{2,1,0:T(1,128)S(1)}, u32[]{:S(2)}, u32[]{:S(2)}) async-start(s32[32,1,128]{2,1,0:T(1,128)} %distinct.1), calls=%async_computation | async-start | bytes 32768 | tf_op jit(solution)/shard_map/all_to_all | solution.py:167
  9.0 0.8 %reshape.9 = s32[20,16,16]{2,1,0:T(8,128)S(1)} reshape(s32[20,256]{1,0:T(8,128)} %bitcast.5) | data formatting | bytes 40960 | tf_op jit(solution)/shard_map/reshape | solution.py:184
  9.8 0.0 copy-start.1
  9.8 0.1 copy.7
  9.9 0.0 copy-start.2
  9.9 0.1 reshape.10
  10.1 6.0 %all-to-all-done.refs_0_ = s32[32,1,128]{2,1,0:T(1,128)S(1)} async-done(((s32[32,1,128]{2,1,0:T(1,128)}), s32[32,1,128]{2,1,0:T(1,128)S(1)}, u32[]{:S(2)}, u32[]{:S(2)}) %all-to-all-start) | async-done | bytes 16416 | tf_op jit(solution)/shard_map/all_to_all | solution.py:167
  16.1 0.0 copy-start
  16.1 1.3 %copy-done = bf16[256,20,128]{2,0,1:T(8,128)(2,1)S(1)} copy-done((bf16[256,20,128]{2,0,1:T(8,128)(2,1)S(1)}, bf16[256,20,128]{2,0,1:T(8,128)(2,1)}, u32[]{:S(2)}) %copy-start) | copy-done | bytes 1310744
  17.4 0.0 copy-start.3
  17.4 0.8 %pack.1 = bf16[32,40,128]{2,1,0:T(8,128)(2,1)S(1)} custom-call(s32[32,1,128]{2,1,0:T(1,128)S(1)} %all-to-all-done.refs_0_, s32[32,320]{1,0:T(8,128)S(1)} %reshape.11.refs_1_, bf16[20,256,128]{2,1,0:T(8,128)(2,1)S(1)} %bitcast.3), custom_call_target="tpu_custom_call" | custom-call | tf_op jit(solution)/shard_map/pack/pallas_call | solution.py:186
  18.2 14.3 %all_to_all.10.packed_ref = bf16[32,40,128]{2,1,0:T(8,128)(2,1)S(1)} all-to-all(bf16[32,40,128]{2,1,0:T(8,128)(2,1)S(1)} %pack.1), channel_id=1, replica_groups=mesh['role'=2,'shard'=16] {'role','shard'}, dimensions={0} | all-to-all | bytes 655360 | tf_op jit(solution)/shard_map/all_to_all | solution.py:167
  32.5 0.0 copy-done.1
  32.5 0.0 copy-done.2
  32.5 0.0 copy-done.3
  32.5 7.9 %tower.1 = bf16[8,200,128]{2,1,0:T(8,128)(2,1)} custom-call(bf16[32,40,128]{2,1,0:T(8,128)(2,1)S(1)} %all_to_all.10.packed_ref, bf16[8,200,128]{2,1,0:T(8,128)(2,1)S(1)} %copy-done.1, bf16[256,512]{1,0:T(8,128)(2,1)S(1)} %copy-done.2, bf16[512,128]{1,0:T(8,128)(2,1)S(1)} %copy-done.3), custom_call_target="tpu_custom_call" | custom-call | tf_op jit(solution)/shard_map/tower/pallas_call | solution.py:194
  (2 shorter events, 0.1 us)
Async XLA Ops:
  0.0 0.7 %copy-start.4 = (s32[8,200]{1,0:T(8,128)S(1)}, s32[8,200]{1,0:T(8,128)}, u32[]{:S(2)}) copy-start(s32[8,200]{1,0:T(8,128)} %cat_ref.1) | copy-start | bytes 19204
  1.6 14.4 %all-to-all-start = ((s32[32,1,128]{2,1,0:T(1,128)}), s32[32,1,128]{2,1,0:T(1,128)S(1)}, u32[]{:S(2)}, u32[]{:S(2)}) async-start(s32[32,1,128]{2,1,0:T(1,128)} %distinct.1), calls=%async_computation | async-start | bytes 32768 | tf_op jit(solution)/shard_map/all_to_all | solution.py:167
  9.8 22.7 %copy-start.1 = (bf16[8,200,128]{2,1,0:T(8,128)(2,1)S(1)}, bf16[8,200,128]{2,1,0:T(8,128)(2,1)}, u32[]{:S(2)}) copy-start(bf16[8,200,128]{2,1,0:T(8,128)(2,1)} %cand_ref.1) | copy-start | bytes 1228804
  9.9 22.6 %copy-start.2 = (bf16[256,512]{1,0:T(8,128)(2,1)S(1)}, bf16[256,512]{1,0:T(8,128)(2,1)}, u32[]{:S(2)}) copy-start(bf16[256,512]{1,0:T(8,128)(2,1)} %w_in_ref.1) | copy-start | bytes 786436
  16.1 1.3 %copy-start = (bf16[256,20,128]{2,0,1:T(8,128)(2,1)S(1)}, bf16[256,20,128]{2,0,1:T(8,128)(2,1)}, u32[]{:S(2)}) copy-start(bf16[256,20,128]{2,0,1:T(8,128)(2,1)} %param.6) | copy-start | bytes 3932164
  17.4 15.1 %copy-start.3 = (bf16[512,128]{1,0:T(8,128)(2,1)S(1)}, bf16[512,128]{1,0:T(8,128)(2,1)}, u32[]{:S(2)}) copy-start(bf16[512,128]{1,0:T(8,128)(2,1)} %w_out_ref.1) | copy-start | bytes 393220

commit v4 on v3

--- a/solution.py
+++ b/solution.py
@@ -45,7 +45,8 @@
     out_ref[...] = jnp.broadcast_to(packed.reshape(1, 1, LANES), out_ref.shape)
 
 
-def pack_kernel(wanted_ref, event_ref, history_ref, out_ref, *, own_users):
+def pack_kernel(wanted_ref, event_ref, history_ref, query_ref, out_ref, *, own_users):
+    del query_ref
     devices = wanted_ref.shape[0]
     blocks_events = history_ref.shape[0]
     width = history_ref.shape[2]
@@ -101,9 +102,43 @@
             out_ref[device, rows:, :] = mark.astype(jnp.bfloat16)
 
 
-def tower_kernel(packed_ref, cand_ref, w_in_ref, w_out_ref, out_ref):
-    own_users, cand_count, width = cand_ref.shape
-    pairs = own_users // 2
+def stage_kernel(history_ref, staged_ref, sem):
+    copy = pltpu.make_async_copy(history_ref, staged_ref, sem)
+    copy.start()
+    copy.wait()
+
+
+def query_kernel(cand_ref, query_ref, *, cand_count):
+    width = cand_ref.shape[1]
+    head_of = iota((cand_count, width), 1) // (width // HEADS)
+    for pair in range(query_ref.shape[0]):
+        both = [
+            cand_ref[(2 * pair + member) * cand_count : (2 * pair + member + 1) * cand_count, :].astype(jnp.float32)
+            for member in range(2)
+        ]
+        for member in range(2):
+            parts = [jnp.where(head_of == head, both[member], 0.0) for head in range(HEADS)]
+            query_ref[pair, :, member * width : (member + 1) * width] = jnp.concatenate(parts, axis=0).astype(
+                jnp.bfloat16
+            )
+
+
+def chunks(total, most):
+    best = total
+    for size in range(8, most + 1, 8):
+        if total % size == 0 and (size % 16 == 0 or total % 16):
+            best = size
+    return [(start, best) for start in range(0, total, best)]
+
+
+def tower_kernel(
+    packed_ref, query_ref, cand_ref, w_in_ref, w_out_ref, out_ref,
+    score_ref, weight_ref, sum_ref, interest_ref, hidden_ref, active_ref, result_ref, sems,
+):
+    pairs, head_rows, _ = query_ref.shape
+    cand_count = head_rows // HEADS
+    rows = 2 * cand_count
+    width = cand_ref.shape[1]
     devices = packed_ref.shape[0]
     slots = devices * CAP
     head_size = width // HEADS
@@ -112,51 +147,93 @@
     pick = jnp.where(iota((2 * CAP, LANES), 0) == iota((2 * CAP, LANES), 1), 1.0, 0.0).astype(jnp.bfloat16)
     across = lax.dot_general(pick, marks, (((1,), (1,)), ((), ())), preferred_element_type=jnp.float32)
     marks = marks.astype(jnp.float32)
-    slot_head = iota((slots, width), 1) // head_size
-    head_of = iota((cand_count, width), 1) // head_size
-    w_in = w_in_ref[...]
-    w_out = w_out_ref[...]
+    slot_even = (iota((slots, width), 1) // head_size) % 2 == 0
+    values = {}
+
+    def score(pair):
+        keys = packed_ref[:, pair * CAP : (pair + 1) * CAP, :].reshape(slots, width).astype(jnp.float32)
+        owned = jnp.broadcast_to(marks[:, pair : pair + 1], (slots, width))
+        shared = 1.0 - owned
+        own_keys = (keys * owned, keys * shared)
+        right = jnp.concatenate([part.astype(jnp.bfloat16) for part in own_keys], axis=1)
+        both = ((own_keys[0], owned), (own_keys[1], shared))
+        values[pair] = (
+            jnp.concatenate([jnp.where(slot_even, k, o).astype(jnp.bfloat16) for k, o in both], axis=1),
+            jnp.concatenate([jnp.where(slot_even, o, k).astype(jnp.bfloat16) for k, o in both], axis=1),
+        )
+        score_ref[pair] = lax.dot_general(
+            query_ref[pair], right, (((1,), (1,)), ((), ())), preferred_element_type=jnp.float32
+        )
+
+    def weigh(pair):
+        mark = across[pair : pair + 1, :]
+        bar_first = (1.0 - mark) * BARRED
+        bar_second = mark * BARRED
+        for start, size in chunks(head_rows, 32):
+            scores = score_ref[pair, start : start + size, :]
+            peak_first = jnp.max(scores + bar_first, axis=1, keepdims=True)
+            peak_second = jnp.max(scores + bar_second, axis=1, keepdims=True)
+            peak = jnp.where(mark > 0.5, peak_first, peak_second)
+            weight_ref[pair, start : start + size, :] = jnp.exp2((scores - peak) * scale).astype(jnp.bfloat16)
+
+    def gather(pair):
+        for head in range(HEADS):
+            span = slice(head * cand_count, (head + 1) * cand_count)
+            sum_ref[pair, span, :] = jnp.dot(
+                weight_ref[pair, span, :], values[pair][head % 2], preferred_element_type=jnp.float32
+            )
+
+    def blend(pair):
+        for start, size in chunks(cand_count, 40):
+            head_of = iota((size, width), 1) // head_size
+            for member in range(2):
+                parts = [
+                    sum_ref[
+                        pair,
+                        head * cand_count + start : head * cand_count + start + size,
+                        member * width : (member + 1) * width,
+                    ]
+                    for head in range(HEADS)
+                ]
+                top = parts[0]
+                total = parts[HEADS - 1]
+                for head in range(1, HEADS):
+                    top = jnp.where(head_of == head, parts[head], top)
+                    total = jnp.where(head_of == head, parts[head - 1], total)
+                inverse = pltpu.roll(1.0 / total, width - head_size, 1)
+                interest_ref[pair, member * cand_count + start : member * cand_count + start + size, :] = (
+                    top * inverse
+                )
+
+    def enter(pair):
+        joined = jnp.concatenate(
+            [cand_ref[pair * rows : (pair + 1) * rows, :], interest_ref[pair].astype(jnp.bfloat16)], axis=1
+        )
+        hidden_ref[pair] = jnp.dot(joined, w_in_ref[...], preferred_element_type=jnp.float32)
+
+    def activate(pair):
+        for start, size in chunks(rows, 16):
+            middle = hidden_ref[pair, start : start + size, :] * 0.5
+            active_ref[pair, start : start + size, :] = (middle * jnp.tanh(middle) + middle).astype(jnp.bfloat16)
+
+    def leave(pair):
+        result = jnp.dot(active_ref[pair], w_out_ref[...], preferred_element_type=jnp.float32)
+        result_ref[pair * rows : (pair + 1) * rows, :] = result.astype(jnp.bfloat16)
+        copy_out(pair).start()
+
+    def copy_out(pair):
+        span = pl.ds(pair * rows, rows)
+        return pltpu.make_async_copy(result_ref.at[span], out_ref.at[span], sems.at[pair])
+
+    stages = (score, weigh, gather, blend, enter, activate, leave)
+    lag = 2
+    for tick in range(len(stages) + lag * (pairs - 1)):
+        for pair in range(pairs):
+            stage = tick - lag * pair
+            if 0 <= stage < len(stages):
+                stages[stage](pair)
     for pair in range(pairs):
-        keys = packed_ref[:, pair * CAP : (pair + 1) * CAP, :].reshape(slots, width).astype(jnp.float32)
-        owned = jnp.broadcast_to(marks[:, pair : pair + 1], (slots, width)) > 0.5
-        own_keys = (jnp.where(owned, keys, 0.0), jnp.where(owned, 0.0, keys))
-        ones = (jnp.where(owned, 1.0, 0.0), jnp.where(owned, 0.0, 1.0))
-        right = jnp.concatenate([part.astype(jnp.bfloat16) for part in own_keys], axis=1)
-        values = []
-        for parity in range(2):
-            mixed = [jnp.where(slot_head % 2 == parity, k, o).astype(jnp.bfloat16) for k, o in zip(own_keys, ones)]
-            values.append(jnp.concatenate(mixed, axis=1))
-        first = jnp.broadcast_to(across[pair : pair + 1, :], (cand_count, slots)) > 0.5
-        cands = [cand_ref[2 * pair + member].astype(jnp.float32) for member in range(2)]
-        tops = [jnp.zeros((cand_count, width), jnp.float32)] * 2
-        totals = [jnp.ones((cand_count, width), jnp.float32)] * 2
-        for head in range(HEADS):
-            left = jnp.concatenate(
-                [jnp.where(head_of == head, c, 0.0).astype(jnp.bfloat16) for c in cands], axis=1
-            )
-            scores = lax.dot_general(left, right, (((1,), (1,)), ((), ())), preferred_element_type=jnp.float32)
-            peak_first = jnp.max(jnp.where(first, scores, BARRED), axis=1, keepdims=True)
-            peak_second = jnp.max(jnp.where(first, BARRED, scores), axis=1, keepdims=True)
-            expo = jnp.exp2((scores - jnp.where(first, peak_first, peak_second)) * scale).astype(jnp.bfloat16)
-            both = jnp.dot(expo, values[head % 2], preferred_element_type=jnp.float32)
-            for member in range(2):
-                part = both[:, member * width : (member + 1) * width]
-                tops[member] = jnp.where(head_of == head, part, tops[member])
-                totals[member] = jnp.where(head_of == head ^ 1, part, totals[member])
-        for member in range(2):
-            inverse = 1.0 / totals[member]
-            inverse = jnp.where(
-                head_of % 2 == 0,
-                pltpu.roll(inverse, width - head_size, 1),
-                pltpu.roll(inverse, head_size, 1),
-            )
-            interest = (tops[member] * inverse).astype(jnp.bfloat16)
-            joined = jnp.concatenate([cand_ref[2 * pair + member], interest], axis=1)
-            hidden = jnp.dot(joined, w_in, preferred_element_type=jnp.float32)
-            middle = hidden * 0.5
-            hidden = (middle * jnp.tanh(middle) + middle).astype(jnp.bfloat16)
-            result = jnp.dot(hidden, w_out, preferred_element_type=jnp.float32)
-            out_ref[2 * pair + member] = result.astype(jnp.bfloat16)
+        copy_out(pair).wait()
 
 
 def near(value):
@@ -172,32 +249,67 @@
     own_users, cand_count, width = candidates.shape
     users, block_events = event_cat.shape
     pairs = own_users // 2
+    resident = pl.BlockSpec(memory_space=pltpu.VMEM)
     wanted = pl.pallas_call(
         distinct_kernel,
-        out_shape=jax.ShapeDtypeStruct((devices, 1, LANES), jnp.int32),
+        out_shape=pltpu.VMEM((devices, 1, LANES), jnp.int32),
+        out_specs=resident,
         compiler_params=pltpu.CompilerParams(vmem_limit_bytes=4 * MEBI),
         name="distinct",
     )(cand_cat)
     wanted = exchange(wanted)
-    resident = pl.BlockSpec(memory_space=pltpu.VMEM)
+    by_event = history.transpose(1, 0, 2)
+    stored = pl.pallas_call(
+        stage_kernel,
+        out_shape=pltpu.VMEM(by_event.shape, jnp.bfloat16),
+        in_specs=[pl.BlockSpec(memory_space=pltpu.HBM)],
+        out_specs=resident,
+        scratch_shapes=[pltpu.SemaphoreType.DMA(())],
+        compiler_params=pltpu.CompilerParams(vmem_limit_bytes=4 * MEBI),
+        name="stage",
+    )(by_event)
+    rows = own_users * cand_count
+    queries = near(candidates.reshape(rows, width))
+    query = pl.pallas_call(
+        lambda *refs: query_kernel(*refs, cand_count=cand_count),
+        out_shape=pltpu.VMEM((pairs, HEADS * cand_count, 2 * width), jnp.bfloat16),
+        in_specs=[resident],
+        out_specs=resident,
+        compiler_params=pltpu.CompilerParams(vmem_limit_bytes=16 * MEBI),
+        name="query",
+    )(queries)
     span = math.lcm(16, own_users)
     grouped = event_cat.T.reshape(block_events, users // span, span).transpose(1, 0, 2)
     grouped = jnp.repeat(grouped.reshape(users // span, block_events * span), span // own_users, axis=0)
     packed = pl.pallas_call(
         lambda *refs: pack_kernel(*refs, own_users=own_users),
-        out_shape=jax.ShapeDtypeStruct((devices, (pairs + 1) * CAP, width), jnp.bfloat16),
-        in_specs=[resident] * 3,
+        out_shape=pltpu.VMEM((devices, (pairs + 1) * CAP, width), jnp.bfloat16),
+        out_specs=resident,
+        in_specs=[resident] * 4,
         compiler_params=pltpu.CompilerParams(vmem_limit_bytes=24 * MEBI),
         name="pack",
-    )(near(wanted), near(grouped), near(history.transpose(1, 0, 2)))
+    )(near(wanted), near(grouped), near(stored), near(query))
     received = exchange(packed)
-    return pl.pallas_call(
+    slots = devices * CAP
+    result = pl.pallas_call(
         tower_kernel,
-        out_shape=jax.ShapeDtypeStruct(candidates.shape, jnp.bfloat16),
-        in_specs=[resident] * 4,
-        compiler_params=pltpu.CompilerParams(vmem_limit_bytes=32 * MEBI),
+        out_shape=jax.ShapeDtypeStruct((rows, width), jnp.bfloat16),
+        in_specs=[resident] * 5,
+        out_specs=pl.BlockSpec(memory_space=pltpu.HBM),
+        scratch_shapes=[
+            pltpu.VMEM((pairs, HEADS * cand_count, slots), jnp.float32),
+            pltpu.VMEM((pairs, HEADS * cand_count, slots), jnp.bfloat16),
+            pltpu.VMEM((pairs, HEADS * cand_count, 2 * width), jnp.float32),
+            pltpu.VMEM((pairs, 2 * cand_count, width), jnp.float32),
+            pltpu.VMEM((pairs, 2 * cand_count, w_input.shape[1]), jnp.float32),
+            pltpu.VMEM((pairs, 2 * cand_count, w_input.shape[1]), jnp.bfloat16),
+            pltpu.VMEM((rows, width), jnp.bfloat16),
+            pltpu.SemaphoreType.DMA((pairs,)),
+        ],
+        compiler_params=pltpu.CompilerParams(vmem_limit_bytes=40 * MEBI),
         name="tower",
-    )(near(received), near(candidates), near(w_input), near(w_output))
+    )(near(received), near(query), queries, near(w_input), near(w_output))
+    return result.reshape(own_users, cand_count, width)
 
 
 def solution(mesh):

time: 40.7 us -> 36.1 us (0.89)
  Pallas kernels: 9.62 us -> 6.12 us
  waiting for transfers between devices: 5.97 us -> 3.41 us
  local copies, waits for them, and re-layouts: 3.08 us -> 3.96 us
  blocking collectives: 14.3 us -> 14.8 us
    pallas_call x2 -> x4, Pallas kernels: 8.81 us -> 5.31 us  [the longest x1 4.03 us: local(): pl.pallas_call(tower_kernel, out_shape=jax.ShapeDtypeStruct((rows, width)...]
    all_to_all x1, waiting for transfers between devices: 5.97 us -> 3.41 us  [exchange(): return lax.all_to_all(parts, AXES, split_axis=0, concat_axis=0, tiled=True)]
    unnamed x10, local copies, waits for them, and re-layouts: 2.03 us -> 2.91 us
    all_to_all x1, blocking collectives: 14.3 us -> 14.8 us  [exchange(): return lax.all_to_all(parts, AXES, split_axis=0, concat_axis=0, tiled=True)]
  transfers between devices with their start and end apart: 1 -> 1, of which waited for: 1 -> 1; matrix products, arithmetic and copies ran while one was open for 3% -> 3% of each run, Pallas kernels for 0% -> 1%
where the time goes in v4:
time: 36.1 us; the launch traced here: 35.7 us
  blocking collectives  14.8 us (41%)
  starting transfers between devices  7.33 us (20%)
  Pallas kernels  6.12 us (17%)
  local copies, waits for them, and re-layouts  3.96 us (11%)
  waiting for transfers between devices  3.41 us (9%)
    all_to_all x1, blocking collectives, exchange(): return lax.all_to_all(parts, AXES, split_axis=0, concat_axis=0, tiled=True)  14.8 us
    all_to_all x1, starting transfers between devices, exchange(): return lax.all_to_all(parts, AXES, split_axis=0, concat_axis=0, tiled=True)  7.33 us
    pallas_call x1, Pallas kernels, local(): pl.pallas_call(tower_kernel, out_shape=jax.ShapeDtypeStruct((rows, width)...  4.03 us
    all_to_all x1, waiting for transfers between devices, exchange(): return lax.all_to_all(parts, AXES, split_axis=0, concat_axis=0, tiled=True)  3.41 us
    unnamed x10, local copies, waits for them, and re-layouts  2.91 us
    pallas_call x1, Pallas kernels, local(): pl.pallas_call(distinct_kernel, out_shape=pltpu.VMEM((devices, 1, LANES),...  0.94 us
    reshape x1, local copies, waits for them, and re-layouts, local(): event_cat.T.reshape(block_events, users // span, span).transpose(1, 0, 2)  0.84 us
    pallas_call x1, Pallas kernels, local(): pl.pallas_call(lambda *refs: pack_kernel(*refs, own_users=own_users), out...  0.81 us
  transfers between devices with their start and end apart: 1, of which 1 were waited for; matrix products, arithmetic and copies ran while one was open for 3% of the time, Pallas kernels for 1%

profile of v4, /device:TPU:0, one launch (start us, length us, event | category | flops | bytes accessed | tf_op | source)
XLA Modules:
  0.0 35.7 jit_solution(6669083312074326829)
XLA Ops:
  0.0 0.0 copy-start.4
  0.0 0.7 %copy-done.4 = s32[8,200]{1,0:T(8,128)S(1)} copy-done((s32[8,200]{1,0:T(8,128)S(1)}, s32[8,200]{1,0:T(8,128)}, u32[]{:S(2)}) %copy-start.4) | copy-done | bytes 6424
  0.7 0.9 %distinct.1 = s32[32,1,128]{2,1,0:T(1,128)} custom-call(s32[8,200]{1,0:T(8,128)S(1)} %copy-done.4), custom_call_target="tpu_custom_call" | custom-call | tf_op jit(solution)/shard_map/distinct/pallas_call | solution.py:253
  1.6 7.3 %all-to-all-start = ((s32[32,1,128]{2,1,0:T(1,128)}), s32[32,1,128]{2,1,0:T(1,128)S(1)}, u32[]{:S(2)}, u32[]{:S(2)}) async-start(s32[32,1,128]{2,1,0:T(1,128)} %distinct.1), calls=%async_computation | async-start | bytes 32768 | tf_op jit(solution)/shard_map/all_to_all | solution.py:244
  9.0 0.8 %reshape.15 = s32[20,16,16]{2,1,0:T(8,128)S(1)} reshape(s32[20,256]{1,0:T(8,128)} %bitcast.9) | data formatting | bytes 40960 | tf_op jit(solution)/shard_map/reshape | solution.py:282
  9.8 0.1 copy.7
  9.9 0.1 reshape.16
  10.1 0.0 copy-start.1
  10.1 1.3 %copy-done.1 = bf16[256,20,128]{2,0,1:T(8,128)(2,1)S(1)} copy-done((bf16[256,20,128]{2,0,1:T(8,128)(2,1)S(1)}, bf16[256,20,128]{2,0,1:T(8,128)(2,1)}, u32[]{:S(2)}) %copy-start.1) | copy-done | bytes 1310744
  11.4 0.0 copy-start
  11.4 0.1 stage.1.refs_2_
  11.5 0.9 %copy-done = bf16[8,200,128]{2,1,0:T(8,128)(2,1)S(1)} copy-done((bf16[8,200,128]{2,1,0:T(8,128)(2,1)S(1)}, bf16[8,200,128]{2,1,0:T(8,128)(2,1)}, u32[]{:S(2)}) %copy-start) | copy-done | bytes 409624
  12.4 0.2 query.1.refs_3_.query_ref
  12.6 0.0 copy-start.3
  12.6 3.4 %all-to-all-done.refs_0_ = s32[32,1,128]{2,1,0:T(1,128)S(1)} async-done(((s32[32,1,128]{2,1,0:T(1,128)}), s32[32,1,128]{2,1,0:T(1,128)S(1)}, u32[]{:S(2)}, u32[]{:S(2)}) %all-to-all-start) | async-done | bytes 16416 | tf_op jit(solution)/shard_map/all_to_all | solution.py:244
  16.1 0.0 copy-start.2
  16.1 0.8 %pack.1 = bf16[32,40,128]{2,1,0:T(8,128)(2,1)S(1)} custom-call(s32[32,1,128]{2,1,0:T(1,128)S(1)} %all-to-all-done.refs_0_, s32[32,320]{1,0:T(8,128)S(1)} %reshape.17.refs_1_, bf16[20,256,128]{2,1,0:T(8,128)(2,1)S(1)} %stage.1.refs_2_, bf16[4,800,256]{2,1,0:T(8,128)(2,1)S(1)} %query.1.refs_3_.query_ref), custom_call_target="tpu_custom_call" | custom-call | tf_op jit(solution)/shard_map/pack/pallas_call | solution.py:284
  16.9 14.8 %all_to_all.10.packed_ref = bf16[32,40,128]{2,1,0:T(8,128)(2,1)S(1)} all-to-all(bf16[32,40,128]{2,1,0:T(8,128)(2,1)S(1)} %pack.1), channel_id=1, replica_groups=mesh['role'=2,'shard'=16] {'role','shard'}, dimensions={0} | all-to-all | bytes 655360 | tf_op jit(solution)/shard_map/all_to_all | solution.py:244
  31.7 0.0 copy-done.3
  31.7 0.0 copy-done.2
  31.7 4.0 %tower.1 = bf16[1600,128]{1,0:T(8,128)(2,1)} custom-call(bf16[32,40,128]{2,1,0:T(8,128)(2,1)S(1)} %all_to_all.10.packed_ref, bf16[4,800,256]{2,1,0:T(8,128)(2,1)S(1)} %query.1.refs_3_.query_ref, bf16[1600,128]{1,0:T(8,128)(2,1)S(1)} %bitcast.6, bf16[256,512]{1,0:T(8,128)(2,1)S(1)} %copy-done.2, bf16[512,128]{1,0:T(8,128)(2,1)S(1)} %copy-done.3), custom_call_target="tpu_custom_call" | custom-call | tf_op jit(solution)/shard_map/tower/pallas_call | solution.py:294
  (2 shorter events, 0.1 us)
Async XLA Ops:
  0.0 0.7 %copy-start.4 = (s32[8,200]{1,0:T(8,128)S(1)}, s32[8,200]{1,0:T(8,128)}, u32[]{:S(2)}) copy-start(s32[8,200]{1,0:T(8,128)} %cat_ref.1) | copy-start | bytes 19204
  1.6 14.4 %all-to-all-start = ((s32[32,1,128]{2,1,0:T(1,128)}), s32[32,1,128]{2,1,0:T(1,128)S(1)}, u32[]{:S(2)}, u32[]{:S(2)}) async-start(s32[32,1,128]{2,1,0:T(1,128)} %distinct.1), calls=%async_computation | async-start | bytes 32768 | tf_op jit(solution)/shard_map/all_to_all | solution.py:244
  10.1 1.3 %copy-start.1 = (bf16[256,20,128]{2,0,1:T(8,128)(2,1)S(1)}, bf16[256,20,128]{2,0,1:T(8,128)(2,1)}, u32[]{:S(2)}) copy-start(bf16[256,20,128]{2,0,1:T(8,128)(2,1)} %param.6) | copy-start | bytes 3932164
  11.4 1.0 %copy-start = (bf16[8,200,128]{2,1,0:T(8,128)(2,1)S(1)}, bf16[8,200,128]{2,1,0:T(8,128)(2,1)}, u32[]{:S(2)}) copy-start(bf16[8,200,128]{2,1,0:T(8,128)(2,1)} %param.8) | copy-start | bytes 1228804
  12.6 19.1 %copy-start.3 = (bf16[512,128]{1,0:T(8,128)(2,1)S(1)}, bf16[512,128]{1,0:T(8,128)(2,1)}, u32[]{:S(2)}) copy-start(bf16[512,128]{1,0:T(8,128)(2,1)} %w_out_ref.1) | copy-start | bytes 393220
  16.1 15.7 %copy-start.2 = (bf16[256,512]{1,0:T(8,128)(2,1)S(1)}, bf16[256,512]{1,0:T(8,128)(2,1)}, u32[]{:S(2)}) copy-start(bf16[256,512]{1,0:T(8,128)(2,1)} %w_in_ref.1) | copy-start | bytes 786436

commit v5 on v4

--- a/solution.py
+++ b/solution.py
@@ -14,6 +14,7 @@
 FINE = 8
 BARRED = -1e30
 MEBI = 1 << 20
+STREAMS = 5
 AXES = ("role", "shard")
 
 
@@ -45,8 +46,7 @@
     out_ref[...] = jnp.broadcast_to(packed.reshape(1, 1, LANES), out_ref.shape)
 
 
-def pack_kernel(wanted_ref, event_ref, history_ref, query_ref, out_ref, *, own_users):
-    del query_ref
+def pack_kernel(wanted_ref, event_ref, history_ref, out_ref, *, own_users):
     devices = wanted_ref.shape[0]
     blocks_events = history_ref.shape[0]
     width = history_ref.shape[2]
@@ -59,7 +59,7 @@
     wanted = wanted_ref[:, 0, :].astype(jnp.float32).astype(jnp.bfloat16)
     line = iota((LANES, pad), 0) % half
     mate = iota((LANES, pad), 1) % own_users
-    events = event_ref[...].astype(jnp.float32)
+    events = event_ref[...]
     match = None
     for j in range(QCAT):
         spread = jnp.where(line == j * own_users + mate, 1.0, 0.0).astype(jnp.bfloat16)
@@ -67,8 +67,6 @@
         same = jnp.where(category == events, 1.0, 0.0)
         match = same if match is None else jnp.maximum(match, same)
     position = iota((devices, depth), 1) % span
-    mine = position // own_users == iota((devices, depth), 0) % per_group
-    match = jnp.where(mine, match, 0.0)
     before = iota((depth, pad), 0)
     here = iota((depth, pad), 1)
     user_before = before % span
@@ -102,25 +100,66 @@
             out_ref[device, rows:, :] = mark.astype(jnp.bfloat16)
 
 
-def stage_kernel(history_ref, staged_ref, sem):
-    copy = pltpu.make_async_copy(history_ref, staged_ref, sem)
-    copy.start()
-    copy.wait()
-
-
-def query_kernel(cand_ref, query_ref, *, cand_count):
+def stage_kernel(
+    history_ref, cand_ref, event_ref, stored_ref, query_ref, grouped_ref, cand_scratch, event_scratch, sems, *, own_users
+):
+    event_copy = pltpu.make_async_copy(event_ref, event_scratch, sems.at[0])
+    cand_copy = pltpu.make_async_copy(cand_ref, cand_scratch, sems.at[1])
+    events = history_ref.shape[0]
+    cuts = [events * part // STREAMS for part in range(STREAMS + 1)]
+    history_copies = [
+        pltpu.make_async_copy(
+            history_ref.at[pl.ds(low, high - low)], stored_ref.at[pl.ds(low, high - low)], sems.at[2 + part]
+        )
+        for part, (low, high) in enumerate(zip(cuts, cuts[1:]))
+    ]
+    event_copy.start()
+    cand_copy.start()
+    for copy in history_copies:
+        copy.start()
+
+    event_copy.wait()
+    users = event_ref.shape[1]
+    devices = users // own_users
+    depth = grouped_ref.shape[1]
+    span = depth // events
+    fold = LANES // span
+    owner = iota((devices, users), 1) // own_users == iota((devices, users), 0)
+    parts = ([], [])
+    for event in range(events):
+        line = event_scratch[event : event + 1, :]
+        fine = line & (FINE - 1)
+        for part, value in zip(parts, (line - fine, fine)):
+            part.append(jnp.where(owner, value.astype(jnp.float32), 0.0).astype(jnp.bfloat16))
+    spread = jnp.where(iota((users, LANES), 0) % span == iota((users, LANES), 1) % span, 1.0, 0.0).astype(jnp.bfloat16)
+    picked = sum(
+        jnp.dot(jnp.concatenate(part, axis=0), spread, preferred_element_type=jnp.float32) for part in parts
+    )
+    lane = iota((devices, LANES), 1)
+    mine = lane % span // own_users == iota((devices, LANES), 0) % (span // own_users)
+    for first in range(0, events, fold):
+        tile = jnp.full((devices, LANES), -1.0, jnp.float32)
+        for event in range(first, min(first + fold, events)):
+            rows = picked[event * devices : (event + 1) * devices, :]
+            tile = jnp.where(mine & (lane // span == event - first), rows, tile)
+        low = first * span
+        high = min(low + LANES, depth)
+        grouped_ref[:, low:high] = tile[:, : high - low]
+
+    cand_copy.wait()
     width = cand_ref.shape[1]
+    cand_count = query_ref.shape[1] // HEADS
     head_of = iota((cand_count, width), 1) // (width // HEADS)
     for pair in range(query_ref.shape[0]):
-        both = [
-            cand_ref[(2 * pair + member) * cand_count : (2 * pair + member + 1) * cand_count, :].astype(jnp.float32)
-            for member in range(2)
-        ]
         for member in range(2):
-            parts = [jnp.where(head_of == head, both[member], 0.0) for head in range(HEADS)]
-            query_ref[pair, :, member * width : (member + 1) * width] = jnp.concatenate(parts, axis=0).astype(
+            start = (2 * pair + member) * cand_count
+            cands = cand_scratch[start : start + cand_count, :].astype(jnp.float32)
+            heads = [jnp.where(head_of == head, cands, 0.0) for head in range(HEADS)]
+            query_ref[pair, :, member * width : (member + 1) * width] = jnp.concatenate(heads, axis=0).astype(
                 jnp.bfloat16
             )
+    for copy in history_copies:
+        copy.wait()
 
 
 def chunks(total, most):
@@ -259,36 +298,35 @@
     )(cand_cat)
     wanted = exchange(wanted)
     by_event = history.transpose(1, 0, 2)
-    stored = pl.pallas_call(
-        stage_kernel,
-        out_shape=pltpu.VMEM(by_event.shape, jnp.bfloat16),
-        in_specs=[pl.BlockSpec(memory_space=pltpu.HBM)],
-        out_specs=resident,
-        scratch_shapes=[pltpu.SemaphoreType.DMA(())],
-        compiler_params=pltpu.CompilerParams(vmem_limit_bytes=4 * MEBI),
+    rows = own_users * cand_count
+    flat_cands = candidates.reshape(rows, width)
+    span = math.lcm(16, own_users)
+    far = pl.BlockSpec(memory_space=pltpu.HBM)
+    stored, query, grouped = pl.pallas_call(
+        lambda *refs: stage_kernel(*refs, own_users=own_users),
+        out_shape=[
+            pltpu.VMEM(by_event.shape, jnp.bfloat16),
+            pltpu.VMEM((pairs, HEADS * cand_count, 2 * width), jnp.bfloat16),
+            pltpu.VMEM((devices, block_events * span), jnp.float32),
+        ],
+        in_specs=[far] * 3,
+        out_specs=[resident] * 3,
+        scratch_shapes=[
+            pltpu.VMEM((rows, width), jnp.bfloat16),
+            pltpu.VMEM((block_events, users), jnp.int32),
+            pltpu.SemaphoreType.DMA((2 + STREAMS,)),
+        ],
+        compiler_params=pltpu.CompilerParams(vmem_limit_bytes=24 * MEBI),
         name="stage",
-    )(by_event)
-    rows = own_users * cand_count
-    queries = near(candidates.reshape(rows, width))
-    query = pl.pallas_call(
-        lambda *refs: query_kernel(*refs, cand_count=cand_count),
-        out_shape=pltpu.VMEM((pairs, HEADS * cand_count, 2 * width), jnp.bfloat16),
-        in_specs=[resident],
-        out_specs=resident,
-        compiler_params=pltpu.CompilerParams(vmem_limit_bytes=16 * MEBI),
-        name="query",
-    )(queries)
-    span = math.lcm(16, own_users)
-    grouped = event_cat.T.reshape(block_events, users // span, span).transpose(1, 0, 2)
-    grouped = jnp.repeat(grouped.reshape(users // span, block_events * span), span // own_users, axis=0)
+    )(*[pltpu.with_memory_space_constraint(value, pltpu.HBM) for value in (by_event, flat_cands, event_cat.T)])
     packed = pl.pallas_call(
         lambda *refs: pack_kernel(*refs, own_users=own_users),
         out_shape=pltpu.VMEM((devices, (pairs + 1) * CAP, width), jnp.bfloat16),
         out_specs=resident,
-        in_specs=[resident] * 4,
+        in_specs=[resident] * 3,
         compiler_params=pltpu.CompilerParams(vmem_limit_bytes=24 * MEBI),
         name="pack",
-    )(near(wanted), near(grouped), near(stored), near(query))
+    )(near(wanted), near(grouped), near(stored))
     received = exchange(packed)
     slots = devices * CAP
     result = pl.pallas_call(
@@ -308,7 +346,7 @@
         ],
         compiler_params=pltpu.CompilerParams(vmem_limit_bytes=40 * MEBI),
         name="tower",
-    )(near(received), near(query), queries, near(w_input), near(w_output))
+    )(near(received), near(query), near(flat_cands), near(w_input), near(w_output))
     return result.reshape(own_users, cand_count, width)
 
 

time: 36.1 us -> 35.4 us (0.981)
  local copies, waits for them, and re-layouts: 3.96 us -> 0.71 us
  waiting for transfers between devices: 3.41 us -> 5.58 us
  Pallas kernels: 6.12 us -> 7.25 us
  blocking collectives: 14.8 us -> 14.3 us
    unnamed x10 -> x8, local copies, waits for them, and re-layouts: 2.91 us -> 0.71 us
    all_to_all x1, waiting for transfers between devices: 3.41 us -> 5.58 us  [exchange(): return lax.all_to_all(parts, AXES, split_axis=0, concat_axis=0, tiled=True)]
    pallas_call x2 -> x1, Pallas kernels: 0.34 us -> 1.47 us  [local(): pl.pallas_call(lambda *refs: stage_kernel(*refs, own_users=own_users), ou...]
    reshape x3 -> x0, local copies, waits for them, and re-layouts: 0.97 us -> none  [the longest x1 0.84 us: local(): event_cat.T.reshape(block_events, users // span, span).transpose(1, 0, 2)]
    all_to_all x1, blocking collectives: 14.8 us -> 14.3 us  [exchange(): return lax.all_to_all(parts, AXES, split_axis=0, concat_axis=0, tiled=True)]
  transfers between devices with their start and end apart: 1 -> 1, of which waited for: 1 -> 1; matrix products, arithmetic and copies ran while one was open for 3% -> 0% of each run, Pallas kernels for 1% -> 4%
where the time goes in v5:
time: 35.4 us; the launch traced here: 35.2 us
  blocking collectives  14.3 us (40%)
  starting transfers between devices  7.33 us (21%)
  Pallas kernels  7.25 us (20%)
  waiting for transfers between devices  5.58 us (16%)
  local copies, waits for them, and re-layouts  0.71 us (2%)
    all_to_all x1, blocking collectives, exchange(): return lax.all_to_all(parts, AXES, split_axis=0, concat_axis=0, tiled=True)  14.3 us
    all_to_all x1, starting transfers between devices, exchange(): return lax.all_to_all(parts, AXES, split_axis=0, concat_axis=0, tiled=True)  7.33 us
    all_to_all x1, waiting for transfers between devices, exchange(): return lax.all_to_all(parts, AXES, split_axis=0, concat_axis=0, tiled=True)  5.58 us
    pallas_call x1, Pallas kernels, local(): pl.pallas_call(tower_kernel, out_shape=jax.ShapeDtypeStruct((rows, width)...  4.03 us
    pallas_call x1, Pallas kernels, local(): pl.pallas_call(lambda *refs: stage_kernel(*refs, own_users=own_users), ou...  1.47 us
    pallas_call x1, Pallas kernels, local(): pl.pallas_call(distinct_kernel, out_shape=pltpu.VMEM((devices, 1, LANES),...  0.94 us
    pallas_call x1, Pallas kernels, local(): pl.pallas_call(lambda *refs: pack_kernel(*refs, own_users=own_users), out...  0.82 us
    unnamed x8, local copies, waits for them, and re-layouts  0.71 us
  transfers between devices with their start and end apart: 1, of which 1 were waited for; matrix products, arithmetic and copies ran while one was open for 0% of the time, Pallas kernels for 4%

profile of v5, /device:TPU:0, one launch (start us, length us, event | category | flops | bytes accessed | tf_op | source)
XLA Modules:
  0.0 35.2 jit_solution(15763157839903549622)
XLA Ops:
  0.0 0.0 copy-start.3
  0.0 0.7 %copy-done.3 = s32[8,200]{1,0:T(8,128)S(1)} copy-done((s32[8,200]{1,0:T(8,128)S(1)}, s32[8,200]{1,0:T(8,128)}, u32[]{:S(2)}) %copy-start.3) | copy-done | bytes 6424
  0.7 0.9 %distinct.1 = s32[32,1,128]{2,1,0:T(1,128)} custom-call(s32[8,200]{1,0:T(8,128)S(1)} %copy-done.3), custom_call_target="tpu_custom_call" | custom-call | tf_op jit(solution)/shard_map/distinct/pallas_call | solution.py:292
  1.6 7.3 %all-to-all-start = ((s32[32,1,128]{2,1,0:T(1,128)}), s32[32,1,128]{2,1,0:T(1,128)S(1)}, u32[]{:S(2)}, u32[]{:S(2)}) async-start(s32[32,1,128]{2,1,0:T(1,128)} %distinct.1), calls=%async_computation | async-start | bytes 32768 | tf_op jit(solution)/shard_map/all_to_all | solution.py:283
  9.0 1.5 %stage.1 = (bf16[20,256,128]{2,1,0:T(8,128)(2,1)S(1)}, bf16[4,800,256]{2,1,0:T(8,128)(2,1)S(1)}, f32[32,320]{1,0:T(8,128)S(1)}) custom-call(bf16[20,256,128]{2,1,0:T(8,128)(2,1)} %bitcast.6, bf16[1600,128]{1,0:T(8,128)(2,1)} %bitcast.4, s32[20,256]{1,0:T(8,128)} %bitcast.7), custom_call_target="tpu_custom_call" | custom-call | tf_op jit(solution)/shard_map/stage/pallas_call | solution.py:305
  10.4 0.0 copy-start
  10.5 0.0 copy-start.2
  10.5 5.6 %all-to-all-done.refs_0_ = s32[32,1,128]{2,1,0:T(1,128)S(1)} async-done(((s32[32,1,128]{2,1,0:T(1,128)}), s32[32,1,128]{2,1,0:T(1,128)S(1)}, u32[]{:S(2)}, u32[]{:S(2)}) %all-to-all-start) | async-done | bytes 16416 | tf_op jit(solution)/shard_map/all_to_all | solution.py:283
  16.1 0.0 copy-start.1
  16.1 0.8 %pack.1 = bf16[32,40,128]{2,1,0:T(8,128)(2,1)S(1)} custom-call(s32[32,1,128]{2,1,0:T(1,128)S(1)} %all-to-all-done.refs_0_, f32[32,320]{1,0:T(8,128)S(1)} %get-tuple-element.8.refs_1_, bf16[20,256,128]{2,1,0:T(8,128)(2,1)S(1)} %get-tuple-element.9.refs_2_), custom_call_target="tpu_custom_call" | custom-call | tf_op jit(solution)/shard_map/pack/pallas_call | solution.py:322
  16.9 14.3 %all_to_all.10.packed_ref = bf16[32,40,128]{2,1,0:T(8,128)(2,1)S(1)} all-to-all(bf16[32,40,128]{2,1,0:T(8,128)(2,1)S(1)} %pack.1), channel_id=1, replica_groups=mesh['role'=2,'shard'=16] {'role','shard'}, dimensions={0} | all-to-all | bytes 655360 | tf_op jit(solution)/shard_map/all_to_all | solution.py:283
  31.2 0.0 copy-done
  31.2 0.0 copy-done.2
  31.2 0.0 copy-done.1
  31.2 4.0 %tower.1 = bf16[1600,128]{1,0:T(8,128)(2,1)} custom-call(bf16[32,40,128]{2,1,0:T(8,128)(2,1)S(1)} %all_to_all.10.packed_ref, bf16[4,800,256]{2,1,0:T(8,128)(2,1)S(1)} %get-tuple-element.10.query_ref, bf16[1600,128]{1,0:T(8,128)(2,1)S(1)} %bitcast.5, bf16[256,512]{1,0:T(8,128)(2,1)S(1)} %copy-done.1, bf16[512,128]{1,0:T(8,128)(2,1)S(1)} %copy-done.2), custom_call_target="tpu_custom_call" | custom-call | tf_op jit(solution)/shard_map/tower/pallas_call | solution.py:332
Async XLA Ops:
  0.0 0.7 %copy-start.3 = (s32[8,200]{1,0:T(8,128)S(1)}, s32[8,200]{1,0:T(8,128)}, u32[]{:S(2)}) copy-start(s32[8,200]{1,0:T(8,128)} %cat_ref.1) | copy-start | bytes 19204
  1.6 14.4 %all-to-all-start = ((s32[32,1,128]{2,1,0:T(1,128)}), s32[32,1,128]{2,1,0:T(1,128)S(1)}, u32[]{:S(2)}, u32[]{:S(2)}) async-start(s32[32,1,128]{2,1,0:T(1,128)} %distinct.1), calls=%async_computation | async-start | bytes 32768 | tf_op jit(solution)/shard_map/all_to_all | solution.py:283
  10.4 20.7 %copy-start = (bf16[8,200,128]{2,1,0:T(8,128)(2,1)S(1)}, bf16[8,200,128]{2,1,0:T(8,128)(2,1)}, u32[]{:S(2)}) copy-start(bf16[8,200,128]{2,1,0:T(8,128)(2,1)} %param.8) | copy-start | bytes 1228804
  10.5 20.7 %copy-start.2 = (bf16[512,128]{1,0:T(8,128)(2,1)S(1)}, bf16[512,128]{1,0:T(8,128)(2,1)}, u32[]{:S(2)}) copy-start(bf16[512,128]{1,0:T(8,128)(2,1)} %w_out_ref.1) | copy-start | bytes 393220
  16.1 15.1 %copy-start.1 = (bf16[256,512]{1,0:T(8,128)(2,1)S(1)}, bf16[256,512]{1,0:T(8,128)(2,1)}, u32[]{:S(2)}) copy-start(bf16[256,512]{1,0:T(8,128)(2,1)} %w_in_ref.1) | copy-start | bytes 786436

commit v6 on v5

--- a/solution.py
+++ b/solution.py
@@ -12,6 +12,7 @@
 QCAT = 8
 LANES = 128
 FINE = 8
+HEAD_ORDER = (*range(0, HEADS, 2), *range(1, HEADS, 2))
 BARRED = -1e30
 MEBI = 1 << 20
 STREAMS = 5
@@ -154,7 +155,7 @@
         for member in range(2):
             start = (2 * pair + member) * cand_count
             cands = cand_scratch[start : start + cand_count, :].astype(jnp.float32)
-            heads = [jnp.where(head_of == head, cands, 0.0) for head in range(HEADS)]
+            heads = [jnp.where(head_of == head, cands, 0.0) for head in HEAD_ORDER]
             query_ref[pair, :, member * width : (member + 1) * width] = jnp.concatenate(heads, axis=0).astype(
                 jnp.bfloat16
             )
@@ -172,7 +173,7 @@
 
 def tower_kernel(
     packed_ref, query_ref, cand_ref, w_in_ref, w_out_ref, out_ref,
-    score_ref, weight_ref, sum_ref, interest_ref, hidden_ref, active_ref, result_ref, sems,
+    score_ref, weight_ref, sum_ref, interest_ref, hidden_ref, active_ref, half_ref, result_ref, sems,
 ):
     pairs, head_rows, _ = query_ref.shape
     cand_count = head_rows // HEADS
@@ -186,19 +187,20 @@
     pick = jnp.where(iota((2 * CAP, LANES), 0) == iota((2 * CAP, LANES), 1), 1.0, 0.0).astype(jnp.bfloat16)
     across = lax.dot_general(pick, marks, (((1,), (1,)), ((), ())), preferred_element_type=jnp.float32)
     marks = marks.astype(jnp.float32)
-    slot_even = (iota((slots, width), 1) // head_size) % 2 == 0
+    slot_even = ((iota((slots, width), 1) // head_size) % 2).astype(jnp.float32).astype(jnp.bfloat16) == 0
     values = {}
+    half_ref[...] = w_in_ref[...] * 0.5
 
     def score(pair):
-        keys = packed_ref[:, pair * CAP : (pair + 1) * CAP, :].reshape(slots, width).astype(jnp.float32)
-        owned = jnp.broadcast_to(marks[:, pair : pair + 1], (slots, width))
-        shared = 1.0 - owned
+        keys = packed_ref[:, pair * CAP : (pair + 1) * CAP, :].reshape(slots, width)
+        owned = jnp.broadcast_to(marks[:, pair : pair + 1], (slots, width)).astype(jnp.bfloat16)
+        shared = 1 - owned
         own_keys = (keys * owned, keys * shared)
-        right = jnp.concatenate([part.astype(jnp.bfloat16) for part in own_keys], axis=1)
+        right = jnp.concatenate(own_keys, axis=1)
         both = ((own_keys[0], owned), (own_keys[1], shared))
         values[pair] = (
-            jnp.concatenate([jnp.where(slot_even, k, o).astype(jnp.bfloat16) for k, o in both], axis=1),
-            jnp.concatenate([jnp.where(slot_even, o, k).astype(jnp.bfloat16) for k, o in both], axis=1),
+            jnp.concatenate([jnp.where(slot_even, k, o) for k, o in both], axis=1),
+            jnp.concatenate([jnp.where(slot_even, o, k) for k, o in both], axis=1),
         )
         score_ref[pair] = lax.dot_general(
             query_ref[pair], right, (((1,), (1,)), ((), ())), preferred_element_type=jnp.float32
@@ -206,18 +208,19 @@
 
     def weigh(pair):
         mark = across[pair : pair + 1, :]
-        bar_first = (1.0 - mark) * BARRED
-        bar_second = mark * BARRED
-        for start, size in chunks(head_rows, 32):
+        bar_first = ((1.0 - mark) * BARRED).astype(jnp.bfloat16)
+        bar_second = (mark * BARRED).astype(jnp.bfloat16)
+        for start, size in chunks(head_rows, 160):
             scores = score_ref[pair, start : start + size, :]
-            peak_first = jnp.max(scores + bar_first, axis=1, keepdims=True)
-            peak_second = jnp.max(scores + bar_second, axis=1, keepdims=True)
+            rough = scores.astype(jnp.bfloat16)
+            peak_first = jnp.max(rough + bar_first, axis=1, keepdims=True).astype(jnp.float32)
+            peak_second = jnp.max(rough + bar_second, axis=1, keepdims=True).astype(jnp.float32)
             peak = jnp.where(mark > 0.5, peak_first, peak_second)
             weight_ref[pair, start : start + size, :] = jnp.exp2((scores - peak) * scale).astype(jnp.bfloat16)
 
     def gather(pair):
-        for head in range(HEADS):
-            span = slice(head * cand_count, (head + 1) * cand_count)
+        for block, head in enumerate(HEAD_ORDER):
+            span = slice(block * cand_count, (block + 1) * cand_count)
             sum_ref[pair, span, :] = jnp.dot(
                 weight_ref[pair, span, :], values[pair][head % 2], preferred_element_type=jnp.float32
             )
@@ -229,10 +232,10 @@
                 parts = [
                     sum_ref[
                         pair,
-                        head * cand_count + start : head * cand_count + start + size,
+                        block * cand_count + start : block * cand_count + start + size,
                         member * width : (member + 1) * width,
                     ]
-                    for head in range(HEADS)
+                    for block in map(HEAD_ORDER.index, range(HEADS))
                 ]
                 top = parts[0]
                 total = parts[HEADS - 1]
@@ -248,11 +251,11 @@
         joined = jnp.concatenate(
             [cand_ref[pair * rows : (pair + 1) * rows, :], interest_ref[pair].astype(jnp.bfloat16)], axis=1
         )
-        hidden_ref[pair] = jnp.dot(joined, w_in_ref[...], preferred_element_type=jnp.float32)
+        hidden_ref[pair] = jnp.dot(joined, half_ref[...], preferred_element_type=jnp.float32)
 
     def activate(pair):
         for start, size in chunks(rows, 16):
-            middle = hidden_ref[pair, start : start + size, :] * 0.5
+            middle = hidden_ref[pair, start : start + size, :]
             active_ref[pair, start : start + size, :] = (middle * jnp.tanh(middle) + middle).astype(jnp.bfloat16)
 
     def leave(pair):
@@ -265,10 +268,10 @@
         return pltpu.make_async_copy(result_ref.at[span], out_ref.at[span], sems.at[pair])
 
     stages = (score, weigh, gather, blend, enter, activate, leave)
-    lag = 2
-    for tick in range(len(stages) + lag * (pairs - 1)):
+    begins = [pair // 2 * 5 for pair in range(pairs)]
+    for tick in range(len(stages) + begins[-1]):
         for pair in range(pairs):
-            stage = tick - lag * pair
+            stage = tick - begins[pair]
             if 0 <= stage < len(stages):
                 stages[stage](pair)
     for pair in range(pairs):
@@ -341,6 +344,7 @@
             pltpu.VMEM((pairs, 2 * cand_count, width), jnp.float32),
             pltpu.VMEM((pairs, 2 * cand_count, w_input.shape[1]), jnp.float32),
             pltpu.VMEM((pairs, 2 * cand_count, w_input.shape[1]), jnp.bfloat16),
+            pltpu.VMEM(w_input.shape, jnp.bfloat16),
             pltpu.VMEM((rows, width), jnp.bfloat16),
             pltpu.SemaphoreType.DMA((pairs,)),
         ],

time: 35.4 us -> 34.7 us (0.980)
  Pallas kernels: 7.25 us -> 6.51 us
    pallas_call x1, Pallas kernels: 4.03 us -> 3.29 us  [local(): pl.pallas_call(tower_kernel, out_shape=jax.ShapeDtypeStruct((rows, width)...]
where the time goes in v6:
time: 34.7 us; the launch traced here: 34.5 us
  blocking collectives  14.3 us (41%)
  starting transfers between devices  7.33 us (21%)
  Pallas kernels  6.51 us (19%)
  waiting for transfers between devices  5.58 us (16%)
  local copies, waits for them, and re-layouts  0.71 us (2%)
    all_to_all x1, blocking collectives, exchange(): return lax.all_to_all(parts, AXES, split_axis=0, concat_axis=0, tiled=True)  14.3 us
    all_to_all x1, starting transfers between devices, exchange(): return lax.all_to_all(parts, AXES, split_axis=0, concat_axis=0, tiled=True)  7.33 us
    all_to_all x1, waiting for transfers between devices, exchange(): return lax.all_to_all(parts, AXES, split_axis=0, concat_axis=0, tiled=True)  5.58 us
    pallas_call x1, Pallas kernels, local(): pl.pallas_call(tower_kernel, out_shape=jax.ShapeDtypeStruct((rows, width)...  3.29 us
    pallas_call x1, Pallas kernels, local(): pl.pallas_call(lambda *refs: stage_kernel(*refs, own_users=own_users), ou...  1.47 us
    pallas_call x1, Pallas kernels, local(): pl.pallas_call(distinct_kernel, out_shape=pltpu.VMEM((devices, 1, LANES),...  0.94 us
    pallas_call x1, Pallas kernels, local(): pl.pallas_call(lambda *refs: pack_kernel(*refs, own_users=own_users), out...  0.82 us
    unnamed x8, local copies, waits for them, and re-layouts  0.71 us
  transfers between devices with their start and end apart: 1, of which 1 were waited for; matrix products, arithmetic and copies ran while one was open for 0% of the time, Pallas kernels for 4%

profile of v6, /device:TPU:0, one launch (start us, length us, event | category | flops | bytes accessed | tf_op | source)
XLA Modules:
  0.0 34.5 jit_solution(17334084937747123890)
XLA Ops:
  0.0 0.0 copy-start.3
  0.0 0.7 %copy-done.3 = s32[8,200]{1,0:T(8,128)S(1)} copy-done((s32[8,200]{1,0:T(8,128)S(1)}, s32[8,200]{1,0:T(8,128)}, u32[]{:S(2)}) %copy-start.3) | copy-done | bytes 6424
  0.7 0.9 %distinct.1 = s32[32,1,128]{2,1,0:T(1,128)} custom-call(s32[8,200]{1,0:T(8,128)S(1)} %copy-done.3), custom_call_target="tpu_custom_call" | custom-call | tf_op jit(solution)/shard_map/distinct/pallas_call | solution.py:295
  1.6 7.3 %all-to-all-start = ((s32[32,1,128]{2,1,0:T(1,128)}), s32[32,1,128]{2,1,0:T(1,128)S(1)}, u32[]{:S(2)}, u32[]{:S(2)}) async-start(s32[32,1,128]{2,1,0:T(1,128)} %distinct.1), calls=%async_computation | async-start | bytes 32768 | tf_op jit(solution)/shard_map/all_to_all | solution.py:286
  9.0 1.5 %stage.1 = (bf16[20,256,128]{2,1,0:T(8,128)(2,1)S(1)}, bf16[4,800,256]{2,1,0:T(8,128)(2,1)S(1)}, f32[32,320]{1,0:T(8,128)S(1)}) custom-call(bf16[20,256,128]{2,1,0:T(8,128)(2,1)} %bitcast.6, bf16[1600,128]{1,0:T(8,128)(2,1)} %bitcast.4, s32[20,256]{1,0:T(8,128)} %bitcast.7), custom_call_target="tpu_custom_call" | custom-call | tf_op jit(solution)/shard_map/stage/pallas_call | solution.py:308
  10.4 0.0 copy-start
  10.5 0.0 copy-start.2
  10.5 5.6 %all-to-all-done.refs_0_ = s32[32,1,128]{2,1,0:T(1,128)S(1)} async-done(((s32[32,1,128]{2,1,0:T(1,128)}), s32[32,1,128]{2,1,0:T(1,128)S(1)}, u32[]{:S(2)}, u32[]{:S(2)}) %all-to-all-start) | async-done | bytes 16416 | tf_op jit(solution)/shard_map/all_to_all | solution.py:286
  16.1 0.0 copy-start.1
  16.1 0.8 %pack.1 = bf16[32,40,128]{2,1,0:T(8,128)(2,1)S(1)} custom-call(s32[32,1,128]{2,1,0:T(1,128)S(1)} %all-to-all-done.refs_0_, f32[32,320]{1,0:T(8,128)S(1)} %get-tuple-element.8.refs_1_, bf16[20,256,128]{2,1,0:T(8,128)(2,1)S(1)} %get-tuple-element.9.refs_2_), custom_call_target="tpu_custom_call" | custom-call | tf_op jit(solution)/shard_map/pack/pallas_call | solution.py:325
  16.9 14.3 %all_to_all.10.packed_ref = bf16[32,40,128]{2,1,0:T(8,128)(2,1)S(1)} all-to-all(bf16[32,40,128]{2,1,0:T(8,128)(2,1)S(1)} %pack.1), channel_id=1, replica_groups=mesh['role'=2,'shard'=16] {'role','shard'}, dimensions={0} | all-to-all | bytes 655360 | tf_op jit(solution)/shard_map/all_to_all | solution.py:286
  31.2 0.0 copy-done
  31.2 0.0 copy-done.2
  31.2 0.0 copy-done.1
  31.2 3.3 %tower.1 = bf16[1600,128]{1,0:T(8,128)(2,1)} custom-call(bf16[32,40,128]{2,1,0:T(8,128)(2,1)S(1)} %all_to_all.10.packed_ref, bf16[4,800,256]{2,1,0:T(8,128)(2,1)S(1)} %get-tuple-element.10.query_ref, bf16[1600,128]{1,0:T(8,128)(2,1)S(1)} %bitcast.5, bf16[256,512]{1,0:T(8,128)(2,1)S(1)} %copy-done.1, bf16[512,128]{1,0:T(8,128)(2,1)S(1)} %copy-done.2), custom_call_target="tpu_custom_call" | custom-call | tf_op jit(solution)/shard_map/tower/pallas_call | solution.py:335
Async XLA Ops:
  0.0 0.7 %copy-start.3 = (s32[8,200]{1,0:T(8,128)S(1)}, s32[8,200]{1,0:T(8,128)}, u32[]{:S(2)}) copy-start(s32[8,200]{1,0:T(8,128)} %cat_ref.1) | copy-start | bytes 19204
  1.6 14.4 %all-to-all-start = ((s32[32,1,128]{2,1,0:T(1,128)}), s32[32,1,128]{2,1,0:T(1,128)S(1)}, u32[]{:S(2)}, u32[]{:S(2)}) async-start(s32[32,1,128]{2,1,0:T(1,128)} %distinct.1), calls=%async_computation | async-start | bytes 32768 | tf_op jit(solution)/shard_map/all_to_all | solution.py:286
  10.4 20.7 %copy-start = (bf16[8,200,128]{2,1,0:T(8,128)(2,1)S(1)}, bf16[8,200,128]{2,1,0:T(8,128)(2,1)}, u32[]{:S(2)}) copy-start(bf16[8,200,128]{2,1,0:T(8,128)(2,1)} %param.8) | copy-start | bytes 1228804
  10.5 20.7 %copy-start.2 = (bf16[512,128]{1,0:T(8,128)(2,1)S(1)}, bf16[512,128]{1,0:T(8,128)(2,1)}, u32[]{:S(2)}) copy-start(bf16[512,128]{1,0:T(8,128)(2,1)} %w_out_ref.1) | copy-start | bytes 393220
  16.1 15.1 %copy-start.1 = (bf16[256,512]{1,0:T(8,128)(2,1)S(1)}, bf16[256,512]{1,0:T(8,128)(2,1)}, u32[]{:S(2)}) copy-start(bf16[256,512]{1,0:T(8,128)(2,1)} %w_in_ref.1) | copy-start | bytes 786436

commit v7 on v6

--- a/solution.py
+++ b/solution.py
@@ -16,6 +16,7 @@
 BARRED = -1e30
 MEBI = 1 << 20
 STREAMS = 5
+TILE = 2
 AXES = ("role", "shard")
 
 
@@ -85,7 +86,6 @@
     lead = jnp.dot(matched, leading, preferred_element_type=jnp.float32)
     rows = pairs * CAP
     row = iota((rows, depth), 0).astype(jnp.float32)
-    rank = iota((CAP, LANES), 0).astype(jnp.float32)
     for group in range(devices // per_group):
         stored = history_ref[:, group * span : (group + 1) * span, :].reshape(depth, width)
         picks = []
@@ -93,12 +93,13 @@
             device = group * per_group + member
             picks.append(jnp.where(row == code[device : device + 1, :], 1.0, 0.0).astype(jnp.bfloat16))
         packed = jnp.dot(jnp.concatenate(picks, axis=0), stored, preferred_element_type=jnp.float32)
-        packed = packed.astype(jnp.bfloat16)
         for member in range(per_group):
             device = group * per_group + member
-            out_ref[device, :rows, :] = packed[member * rows : (member + 1) * rows, :]
-            mark = jnp.where(rank < lead[device : device + 1, :], 1.0, 0.0)
-            out_ref[device, rows:, :] = mark.astype(jnp.bfloat16)
+            block = packed[member * rows : (member + 1) * rows, :].astype(jnp.bfloat16)
+            out_ref[device, : rows // TILE] = block.reshape(rows // TILE, TILE, width)
+            out_ref[device, rows // TILE] = jnp.broadcast_to(lead[device : device + 1, :], (TILE, LANES)).astype(
+                jnp.bfloat16
+            )
 
 
 def stage_kernel(
@@ -183,16 +184,20 @@
     slots = devices * CAP
     head_size = width // HEADS
     scale = math.log2(math.e) * head_size ** (-0.5)
-    marks = packed_ref[:, pairs * CAP :, :].reshape(slots, LANES)
+    lead = packed_ref[:, pairs * CAP // TILE].astype(jnp.float32)[:, :1, :]
+    rank = iota((devices, CAP, LANES), 1).astype(jnp.float32)
+    marks = jnp.where(rank < jnp.broadcast_to(lead, (devices, CAP, LANES)), 1.0, 0.0).reshape(slots, LANES)
     pick = jnp.where(iota((2 * CAP, LANES), 0) == iota((2 * CAP, LANES), 1), 1.0, 0.0).astype(jnp.bfloat16)
-    across = lax.dot_general(pick, marks, (((1,), (1,)), ((), ())), preferred_element_type=jnp.float32)
-    marks = marks.astype(jnp.float32)
+    across = lax.dot_general(
+        pick, marks.astype(jnp.bfloat16), (((1,), (1,)), ((), ())), preferred_element_type=jnp.float32
+    )
     slot_even = ((iota((slots, width), 1) // head_size) % 2).astype(jnp.float32).astype(jnp.bfloat16) == 0
     values = {}
     half_ref[...] = w_in_ref[...] * 0.5
 
     def score(pair):
-        keys = packed_ref[:, pair * CAP : (pair + 1) * CAP, :].reshape(slots, width)
+        keys = packed_ref[:, pair * CAP // TILE : (pair + 1) * CAP // TILE]
+        keys = keys.astype(jnp.float32).reshape(slots, width).astype(jnp.bfloat16)
         owned = jnp.broadcast_to(marks[:, pair : pair + 1], (slots, width)).astype(jnp.bfloat16)
         shared = 1 - owned
         own_keys = (keys * owned, keys * shared)
@@ -324,7 +329,7 @@
     )(*[pltpu.with_memory_space_constraint(value, pltpu.HBM) for value in (by_event, flat_cands, event_cat.T)])
     packed = pl.pallas_call(
         lambda *refs: pack_kernel(*refs, own_users=own_users),
-        out_shape=pltpu.VMEM((devices, (pairs + 1) * CAP, width), jnp.bfloat16),
+        out_shape=pltpu.VMEM((devices, pairs * CAP // TILE + 1, TILE, width), jnp.bfloat16),
         out_specs=resident,
         in_specs=[resident] * 3,
         compiler_params=pltpu.CompilerParams(vmem_limit_bytes=24 * MEBI),

time: 34.7 us -> 33.7 us (0.971)
  blocking collectives: 14.3 us -> 13.3 us
    all_to_all x1, blocking collectives: 14.3 us -> 13.3 us  [exchange(): return lax.all_to_all(parts, AXES, split_axis=0, concat_axis=0, tiled=True)]
where the time goes in v7:
time: 33.7 us; the launch traced here: 33.5 us
  blocking collectives  13.3 us (39%)
  starting transfers between devices  7.33 us (22%)
  Pallas kernels  6.54 us (19%)
  waiting for transfers between devices  5.58 us (17%)
  local copies, waits for them, and re-layouts  0.71 us (2%)
    all_to_all x1, blocking collectives, exchange(): return lax.all_to_all(parts, AXES, split_axis=0, concat_axis=0, tiled=True)  13.3 us
    all_to_all x1, starting transfers between devices, exchange(): return lax.all_to_all(parts, AXES, split_axis=0, concat_axis=0, tiled=True)  7.33 us
    all_to_all x1, waiting for transfers between devices, exchange(): return lax.all_to_all(parts, AXES, split_axis=0, concat_axis=0, tiled=True)  5.58 us
    pallas_call x1, Pallas kernels, local(): pl.pallas_call(tower_kernel, out_shape=jax.ShapeDtypeStruct((rows, width)...  3.3 us
    pallas_call x1, Pallas kernels, local(): pl.pallas_call(lambda *refs: stage_kernel(*refs, own_users=own_users), ou...  1.47 us
    pallas_call x1, Pallas kernels, local(): pl.pallas_call(distinct_kernel, out_shape=pltpu.VMEM((devices, 1, LANES),...  0.94 us
    pallas_call x1, Pallas kernels, local(): pl.pallas_call(lambda *refs: pack_kernel(*refs, own_users=own_users), out...  0.84 us
    unnamed x8, local copies, waits for them, and re-layouts  0.71 us
  transfers between devices with their start and end apart: 1, of which 1 were waited for; matrix products, arithmetic and copies ran while one was open for 0% of the time, Pallas kernels for 4%

profile of v7, /device:TPU:0, one launch (start us, length us, event | category | flops | bytes accessed | tf_op | source)
XLA Modules:
  0.0 33.5 jit_solution(13511364057810303380)
XLA Ops:
  0.0 0.0 copy-start.3
  0.0 0.7 %copy-done.3 = s32[8,200]{1,0:T(8,128)S(1)} copy-done((s32[8,200]{1,0:T(8,128)S(1)}, s32[8,200]{1,0:T(8,128)}, u32[]{:S(2)}) %copy-start.3) | copy-done | bytes 6424
  0.7 0.9 %distinct.1 = s32[32,1,128]{2,1,0:T(1,128)} custom-call(s32[8,200]{1,0:T(8,128)S(1)} %copy-done.3), custom_call_target="tpu_custom_call" | custom-call | tf_op jit(solution)/shard_map/distinct/pallas_call | solution.py:300
  1.6 7.3 %all-to-all-start = ((s32[32,1,128]{2,1,0:T(1,128)}), s32[32,1,128]{2,1,0:T(1,128)S(1)}, u32[]{:S(2)}, u32[]{:S(2)}) async-start(s32[32,1,128]{2,1,0:T(1,128)} %distinct.1), calls=%async_computation | async-start | bytes 32768 | tf_op jit(solution)/shard_map/all_to_all | solution.py:291
  9.0 1.5 %stage.1 = (bf16[20,256,128]{2,1,0:T(8,128)(2,1)S(1)}, bf16[4,800,256]{2,1,0:T(8,128)(2,1)S(1)}, f32[32,320]{1,0:T(8,128)S(1)}) custom-call(bf16[20,256,128]{2,1,0:T(8,128)(2,1)} %bitcast.6, bf16[1600,128]{1,0:T(8,128)(2,1)} %bitcast.4, s32[20,256]{1,0:T(8,128)} %bitcast.7), custom_call_target="tpu_custom_call" | custom-call | tf_op jit(solution)/shard_map/stage/pallas_call | solution.py:313
  10.4 0.0 copy-start
  10.5 0.0 copy-start.2
  10.5 5.6 %all-to-all-done.refs_0_ = s32[32,1,128]{2,1,0:T(1,128)S(1)} async-done(((s32[32,1,128]{2,1,0:T(1,128)}), s32[32,1,128]{2,1,0:T(1,128)S(1)}, u32[]{:S(2)}, u32[]{:S(2)}) %all-to-all-start) | async-done | bytes 16416 | tf_op jit(solution)/shard_map/all_to_all | solution.py:291
  16.1 0.0 copy-start.1
  16.1 0.8 %pack.1 = bf16[32,17,2,128]{3,2,1,0:T(2,128)(2,1)S(1)} custom-call(s32[32,1,128]{2,1,0:T(1,128)S(1)} %all-to-all-done.refs_0_, f32[32,320]{1,0:T(8,128)S(1)} %get-tuple-element.8.refs_1_, bf16[20,256,128]{2,1,0:T(8,128)(2,1)S(1)} %get-tuple-element.9.refs_2_), custom_call_target="tpu_custom_call" | custom-call | tf_op jit(solution)/shard_map/pack/pallas_call | solution.py:330
  16.9 13.3 %all_to_all.10.packed_ref = bf16[32,17,2,128]{3,2,1,0:T(2,128)(2,1)S(1)} all-to-all(bf16[32,17,2,128]{3,2,1,0:T(2,128)(2,1)S(1)} %pack.1), channel_id=1, replica_groups=mesh['role'=2,'shard'=16] {'role','shard'}, dimensions={0} | all-to-all | bytes 557056 | tf_op jit(solution)/shard_map/all_to_all | solution.py:291
  30.1 0.0 copy-done
  30.2 0.0 copy-done.2
  30.2 0.0 copy-done.1
  30.2 3.3 %tower.1 = bf16[1600,128]{1,0:T(8,128)(2,1)} custom-call(bf16[32,17,2,128]{3,2,1,0:T(2,128)(2,1)S(1)} %all_to_all.10.packed_ref, bf16[4,800,256]{2,1,0:T(8,128)(2,1)S(1)} %get-tuple-element.10.query_ref, bf16[1600,128]{1,0:T(8,128)(2,1)S(1)} %bitcast.5, bf16[256,512]{1,0:T(8,128)(2,1)S(1)} %copy-done.1, bf16[512,128]{1,0:T(8,128)(2,1)S(1)} %copy-done.2), custom_call_target="tpu_custom_call" | custom-call | tf_op jit(solution)/shard_map/tower/pallas_call | solution.py:340
Async XLA Ops:
  0.0 0.7 %copy-start.3 = (s32[8,200]{1,0:T(8,128)S(1)}, s32[8,200]{1,0:T(8,128)}, u32[]{:S(2)}) copy-start(s32[8,200]{1,0:T(8,128)} %cat_ref.1) | copy-start | bytes 19204
  1.6 14.4 %all-to-all-start = ((s32[32,1,128]{2,1,0:T(1,128)}), s32[32,1,128]{2,1,0:T(1,128)S(1)}, u32[]{:S(2)}, u32[]{:S(2)}) async-start(s32[32,1,128]{2,1,0:T(1,128)} %distinct.1), calls=%async_computation | async-start | bytes 32768 | tf_op jit(solution)/shard_map/all_to_all | solution.py:291
  10.4 19.7 %copy-start = (bf16[8,200,128]{2,1,0:T(8,128)(2,1)S(1)}, bf16[8,200,128]{2,1,0:T(8,128)(2,1)}, u32[]{:S(2)}) copy-start(bf16[8,200,128]{2,1,0:T(8,128)(2,1)} %param.8) | copy-start | bytes 1228804
  10.5 19.7 %copy-start.2 = (bf16[512,128]{1,0:T(8,128)(2,1)S(1)}, bf16[512,128]{1,0:T(8,128)(2,1)}, u32[]{:S(2)}) copy-start(bf16[512,128]{1,0:T(8,128)(2,1)} %w_out_ref.1) | copy-start | bytes 393220
  16.1 14.1 %copy-start.1 = (bf16[256,512]{1,0:T(8,128)(2,1)S(1)}, bf16[256,512]{1,0:T(8,128)(2,1)}, u32[]{:S(2)}) copy-start(bf16[256,512]{1,0:T(8,128)(2,1)} %w_in_ref.1) | copy-start | bytes 786436

commit v8 on v7

--- a/solution.py
+++ b/solution.py
@@ -48,7 +48,7 @@
     out_ref[...] = jnp.broadcast_to(packed.reshape(1, 1, LANES), out_ref.shape)
 
 
-def pack_kernel(wanted_ref, event_ref, history_ref, out_ref, *, own_users):
+def pack_kernel(wanted_ref, event_ref, history_ref, spread_ref, counted_ref, leading_ref, out_ref, *, own_users):
     devices = wanted_ref.shape[0]
     blocks_events = history_ref.shape[0]
     width = history_ref.shape[2]
@@ -56,42 +56,28 @@
     span = depth // blocks_events
     per_group = span // own_users
     pairs = own_users // 2
-    half = LANES // 2
-    pad = -(-depth // LANES) * LANES
     wanted = wanted_ref[:, 0, :].astype(jnp.float32).astype(jnp.bfloat16)
-    line = iota((LANES, pad), 0) % half
-    mate = iota((LANES, pad), 1) % own_users
     events = event_ref[...]
     match = None
     for j in range(QCAT):
-        spread = jnp.where(line == j * own_users + mate, 1.0, 0.0).astype(jnp.bfloat16)
-        category = jnp.dot(wanted, spread, preferred_element_type=jnp.float32)[:, :depth]
+        category = jnp.dot(wanted, spread_ref[j], preferred_element_type=jnp.float32)[:, :depth]
         same = jnp.where(category == events, 1.0, 0.0)
         match = same if match is None else jnp.maximum(match, same)
     position = iota((devices, depth), 1) % span
-    before = iota((depth, pad), 0)
-    here = iota((depth, pad), 1)
-    user_before = before % span
-    user_here = here % span
-    counted = (user_before == user_here) & (before <= here)
-    counted = counted | ((user_here % 2 == 1) & (user_before == user_here - 1))
-    counted = jnp.where(counted, 1.0, 0.0).astype(jnp.bfloat16)
     matched = match.astype(jnp.bfloat16)
-    place = jnp.dot(matched, counted, preferred_element_type=jnp.float32)[:, :depth]
+    place = jnp.dot(matched, counted_ref[...], preferred_element_type=jnp.float32)[:, :depth]
     pair_base = ((position % own_users) // 2 * CAP - 1).astype(jnp.float32)
     code = jnp.where(match > 0.0, place + pair_base, -1.0)
-    lane = iota((depth, LANES), 1)
-    leading = (lane < pairs) & (iota((depth, LANES), 0) % own_users == 2 * lane)
-    leading = jnp.where(leading, 1.0, 0.0).astype(jnp.bfloat16)
-    lead = jnp.dot(matched, leading, preferred_element_type=jnp.float32)
+    lead = jnp.dot(matched, leading_ref[...], preferred_element_type=jnp.float32)
     rows = pairs * CAP
-    row = iota((rows, depth), 0).astype(jnp.float32)
+    row = iota((rows, depth), 0).astype(jnp.float32).astype(jnp.bfloat16)
     for group in range(devices // per_group):
         stored = history_ref[:, group * span : (group + 1) * span, :].reshape(depth, width)
         picks = []
         for member in range(per_group):
             device = group * per_group + member
-            picks.append(jnp.where(row == code[device : device + 1, :], 1.0, 0.0).astype(jnp.bfloat16))
+            own = jnp.broadcast_to(code[device : device + 1, :], row.shape).astype(jnp.bfloat16)
+            picks.append(jnp.where(row == own, jnp.bfloat16(1), jnp.bfloat16(0)))
         packed = jnp.dot(jnp.concatenate(picks, axis=0), stored, preferred_element_type=jnp.float32)
         for member in range(per_group):
             device = group * per_group + member
@@ -103,7 +89,9 @@
 
 
 def stage_kernel(
-    history_ref, cand_ref, event_ref, stored_ref, query_ref, grouped_ref, cand_scratch, event_scratch, sems, *, own_users
+    history_ref, cand_ref, event_ref,
+    stored_ref, query_ref, grouped_ref, spread_ref, counted_ref, leading_ref,
+    cand_scratch, event_scratch, sems, *, own_users,
 ):
     event_copy = pltpu.make_async_copy(event_ref, event_scratch, sems.at[0])
     cand_copy = pltpu.make_async_copy(cand_ref, cand_scratch, sems.at[1])
@@ -120,11 +108,26 @@
     for copy in history_copies:
         copy.start()
 
+    depth, pad = counted_ref.shape
+    span = depth // events
+    line = iota((LANES, pad), 0) % (LANES // 2)
+    mate = iota((LANES, pad), 1) % own_users
+    for j in range(QCAT):
+        spread_ref[j] = jnp.where(line == j * own_users + mate, 1.0, 0.0).astype(jnp.bfloat16)
+    before = iota((depth, pad), 0)
+    here = iota((depth, pad), 1)
+    user_before = before % span
+    user_here = here % span
+    counted = (user_before == user_here) & (before <= here)
+    counted = counted | ((user_here % 2 == 1) & (user_before == user_here - 1))
+    counted_ref[...] = jnp.where(counted, 1.0, 0.0).astype(jnp.bfloat16)
+    lane = iota((depth, LANES), 1)
+    leading = (lane < own_users // 2) & (iota((depth, LANES), 0) % own_users == 2 * lane)
+    leading_ref[...] = jnp.where(leading, 1.0, 0.0).astype(jnp.bfloat16)
+
     event_copy.wait()
     users = event_ref.shape[1]
     devices = users // own_users
-    depth = grouped_ref.shape[1]
-    span = depth // events
     fold = LANES // span
     owner = iota((devices, users), 1) // own_users == iota((devices, users), 0)
     parts = ([], [])
@@ -224,10 +227,10 @@
             weight_ref[pair, start : start + size, :] = jnp.exp2((scores - peak) * scale).astype(jnp.bfloat16)
 
     def gather(pair):
-        for block, head in enumerate(HEAD_ORDER):
-            span = slice(block * cand_count, (block + 1) * cand_count)
+        for parity in range(2):
+            span = slice(parity * head_rows // 2, (parity + 1) * head_rows // 2)
             sum_ref[pair, span, :] = jnp.dot(
-                weight_ref[pair, span, :], values[pair][head % 2], preferred_element_type=jnp.float32
+                weight_ref[pair, span, :], values[pair][parity], preferred_element_type=jnp.float32
             )
 
     def blend(pair):
@@ -273,7 +276,7 @@
         return pltpu.make_async_copy(result_ref.at[span], out_ref.at[span], sems.at[pair])
 
     stages = (score, weigh, gather, blend, enter, activate, leave)
-    begins = [pair // 2 * 5 for pair in range(pairs)]
+    begins = [pair // 2 * 5 + (pair % 2 if pair > 1 else 0) for pair in range(pairs)]
     for tick in range(len(stages) + begins[-1]):
         for pair in range(pairs):
             stage = tick - begins[pair]
@@ -310,15 +313,20 @@
     flat_cands = candidates.reshape(rows, width)
     span = math.lcm(16, own_users)
     far = pl.BlockSpec(memory_space=pltpu.HBM)
-    stored, query, grouped = pl.pallas_call(
+    depth = block_events * span
+    pad = -(-depth // LANES) * LANES
+    stored, query, grouped, spread, counted, leading = pl.pallas_call(
         lambda *refs: stage_kernel(*refs, own_users=own_users),
         out_shape=[
             pltpu.VMEM(by_event.shape, jnp.bfloat16),
             pltpu.VMEM((pairs, HEADS * cand_count, 2 * width), jnp.bfloat16),
-            pltpu.VMEM((devices, block_events * span), jnp.float32),
+            pltpu.VMEM((devices, depth), jnp.float32),
+            pltpu.VMEM((QCAT, LANES, pad), jnp.bfloat16),
+            pltpu.VMEM((depth, pad), jnp.bfloat16),
+            pltpu.VMEM((depth, LANES), jnp.bfloat16),
         ],
         in_specs=[far] * 3,
-        out_specs=[resident] * 3,
+        out_specs=[resident] * 6,
         scratch_shapes=[
             pltpu.VMEM((rows, width), jnp.bfloat16),
             pltpu.VMEM((block_events, users), jnp.int32),
@@ -331,10 +339,10 @@
         lambda *refs: pack_kernel(*refs, own_users=own_users),
         out_shape=pltpu.VMEM((devices, pairs * CAP // TILE + 1, TILE, width), jnp.bfloat16),
         out_specs=resident,
-        in_specs=[resident] * 3,
+        in_specs=[resident] * 6,
         compiler_params=pltpu.CompilerParams(vmem_limit_bytes=24 * MEBI),
         name="pack",
-    )(near(wanted), near(grouped), near(stored))
+    )(*[near(value) for value in (wanted, grouped, stored, spread, counted, leading)])
     received = exchange(packed)
     slots = devices * CAP
     result = pl.pallas_call(

time: 33.7 us -> 34.7 us (1.030)
  local copies, waits for them, and re-layouts: 0.71 us -> 2.72 us
  waiting for transfers between devices: 5.58 us -> 4.71 us
    unnamed x8 -> x12, local copies, waits for them, and re-layouts: 0.71 us -> 2.72 us
    all_to_all x1, waiting for transfers between devices: 5.58 us -> 4.71 us  [exchange(): return lax.all_to_all(parts, AXES, split_axis=0, concat_axis=0, tiled=True)]
where the time goes in v8:
time: 34.7 us; the launch traced here: 34.4 us
  blocking collectives  13.3 us (38%)
  starting transfers between devices  7.33 us (21%)
  Pallas kernels  6.39 us (18%)
  waiting for transfers between devices  4.71 us (14%)
  local copies, waits for them, and re-layouts  2.72 us (8%)
    all_to_all x1, blocking collectives, exchange(): return lax.all_to_all(parts, AXES, split_axis=0, concat_axis=0, tiled=True)  13.3 us
    all_to_all x1, starting transfers between devices, exchange(): return lax.all_to_all(parts, AXES, split_axis=0, concat_axis=0, tiled=True)  7.33 us
    all_to_all x1, waiting for transfers between devices, exchange(): return lax.all_to_all(parts, AXES, split_axis=0, concat_axis=0, tiled=True)  4.71 us
    pallas_call x1, Pallas kernels, local(): pl.pallas_call(tower_kernel, out_shape=jax.ShapeDtypeStruct((rows, width)...  3.17 us
    unnamed x12, local copies, waits for them, and re-layouts  2.72 us
    pallas_call x1, Pallas kernels, local(): pl.pallas_call(lambda *refs: stage_kernel(*refs, own_users=own_users), ou...  1.47 us
    pallas_call x1, Pallas kernels, local(): pl.pallas_call(distinct_kernel, out_shape=pltpu.VMEM((devices, 1, LANES),...  0.94 us
    pallas_call x1, Pallas kernels, local(): pl.pallas_call(lambda *refs: pack_kernel(*refs, own_users=own_users), out...  0.81 us
  transfers between devices with their start and end apart: 1, of which 1 were waited for; matrix products, arithmetic and copies ran while one was open for 0% of the time, Pallas kernels for 4%

profile of v8, /device:TPU:0, one launch (start us, length us, event | category | flops | bytes accessed | tf_op | source)
XLA Modules:
  0.0 34.4 jit_solution(7493006746752595079)
XLA Ops:
  0.0 0.0 copy-start.5
  0.0 0.7 %copy-done.5 = s32[8,200]{1,0:T(8,128)S(1)} copy-done((s32[8,200]{1,0:T(8,128)S(1)}, s32[8,200]{1,0:T(8,128)}, u32[]{:S(2)}) %copy-start.5) | copy-done | bytes 6424
  0.7 0.9 %distinct.1 = s32[32,1,128]{2,1,0:T(1,128)} custom-call(s32[8,200]{1,0:T(8,128)S(1)} %copy-done.5), custom_call_target="tpu_custom_call" | custom-call | tf_op jit(solution)/shard_map/distinct/pallas_call | solution.py:303
  1.6 7.3 %all-to-all-start = ((s32[32,1,128]{2,1,0:T(1,128)}), s32[32,1,128]{2,1,0:T(1,128)S(1)}, u32[]{:S(2)}, u32[]{:S(2)}) async-start(s32[32,1,128]{2,1,0:T(1,128)} %distinct.1), calls=%async_computation | async-start | bytes 32768 | tf_op jit(solution)/shard_map/all_to_all | solution.py:294
  9.0 1.5 %stage.1 = (bf16[20,256,128]{2,1,0:T(8,128)(2,1)S(1)}, bf16[4,800,256]{2,1,0:T(8,128)(2,1)S(1)}, f32[32,320]{1,0:T(8,128)S(1)}, bf16[8,128,384]{2,1,0:T(8,128)(2...) custom-call(bf16[20,256,128]{2,1,0:T(8,128)(2,1)} %bitcast.6, bf16[1600,128]{1,0:T(8,128)(2,1)} %bitcast.4, ...), custom_call_target="tpu_custom_call" | custom-call | tf_op jit(solution)/shard_map/stage/pallas_call | solution.py:318
  10.4 0.0 copy-start.1
  10.5 0.9 %copy-done.1 = bf16[8,128,384]{2,1,0:T(8,128)(2,1)} copy-done((bf16[8,128,384]{2,1,0:T(8,128)(2,1)}, bf16[8,128,384]{2,1,0:T(8,128)(2,1)S(1)}, u32[]{:S(2)}) %copy-start.1) | copy-done | bytes 786456
  11.3 4.7 %all-to-all-done.refs_0_ = s32[32,1,128]{2,1,0:T(1,128)S(1)} async-done(((s32[32,1,128]{2,1,0:T(1,128)}), s32[32,1,128]{2,1,0:T(1,128)S(1)}, u32[]{:S(2)}, u32[]{:S(2)}) %all-to-all-start) | async-done | bytes 16416 | tf_op jit(solution)/shard_map/all_to_all | solution.py:294
  16.1 0.0 copy-start.2
  16.1 1.1 %copy-done.2 = bf16[8,128,384]{2,1,0:T(8,128)(2,1)S(1)} copy-done((bf16[8,128,384]{2,1,0:T(8,128)(2,1)S(1)}, bf16[8,128,384]{2,1,0:T(8,128)(2,1)}, u32[]{:S(2)}) %copy-start.2) | copy-done | bytes 786456
  17.2 0.0 copy-start
  17.2 0.0 copy-start.3
  17.2 0.0 copy-start.4
  17.2 0.8 %pack.1 = bf16[32,17,2,128]{3,2,1,0:T(2,128)(2,1)S(1)} custom-call(s32[32,1,128]{2,1,0:T(1,128)S(1)} %all-to-all-done.refs_0_, f32[32,320]{1,0:T(8,128)S(1)} %get-tuple-element.11.refs_1_, bf16[20,256,128]{2,1,0:T(8,128)(2,1)S(1)} %get-tuple-element.12.refs_2_, bf16[8,128,384]{2,1,0:T(8,128)(2,1)S(1)} %copy-done.2, ...), custom_call_target="tpu_custom_call" | custom-call | tf_op jit(solution)/shard_map/pack/pallas_call | solution.py:338
  18.0 13.3 %all_to_all.10.packed_ref = bf16[32,17,2,128]{3,2,1,0:T(2,128)(2,1)S(1)} all-to-all(bf16[32,17,2,128]{3,2,1,0:T(2,128)(2,1)S(1)} %pack.1), channel_id=1, replica_groups=mesh['role'=2,'shard'=16] {'role','shard'}, dimensions={0} | all-to-all | bytes 557056 | tf_op jit(solution)/shard_map/all_to_all | solution.py:294
  31.3 0.0 copy-done
  31.3 0.0 copy-done.3
  31.3 0.0 copy-done.4
  31.3 3.2 %tower.1 = bf16[1600,128]{1,0:T(8,128)(2,1)} custom-call(bf16[32,17,2,128]{3,2,1,0:T(2,128)(2,1)S(1)} %all_to_all.10.packed_ref, bf16[4,800,256]{2,1,0:T(8,128)(2,1)S(1)} %get-tuple-element.16.query_ref, bf16[1600,128]{1,0:T(8,128)(2,1)S(1)} %bitcast.5, bf16[256,512]{1,0:T(8,128)(2,1)S(1)} %copy-done.3, bf16[512,128]{1,0:T(8,128)(2,1)S(1)} %copy-done.4), custom_call_target="tpu_custom_call" | custom-call | tf_op jit(solution)/shard_map/tower/pallas_call | solution.py:348
Async XLA Ops:
  0.0 0.7 %copy-start.5 = (s32[8,200]{1,0:T(8,128)S(1)}, s32[8,200]{1,0:T(8,128)}, u32[]{:S(2)}) copy-start(s32[8,200]{1,0:T(8,128)} %cat_ref.1) | copy-start | bytes 19204
  1.6 14.4 %all-to-all-start = ((s32[32,1,128]{2,1,0:T(1,128)}), s32[32,1,128]{2,1,0:T(1,128)S(1)}, u32[]{:S(2)}, u32[]{:S(2)}) async-start(s32[32,1,128]{2,1,0:T(1,128)} %distinct.1), calls=%async_computation | async-start | bytes 32768 | tf_op jit(solution)/shard_map/all_to_all | solution.py:294
  10.4 0.9 %copy-start.1 = (bf16[8,128,384]{2,1,0:T(8,128)(2,1)}, bf16[8,128,384]{2,1,0:T(8,128)(2,1)S(1)}, u32[]{:S(2)}) copy-start(bf16[8,128,384]{2,1,0:T(8,128)(2,1)S(1)} %get-tuple-element.13.refs_3_) | copy-start | bytes 2359300
  16.1 1.1 %copy-start.2 = (bf16[8,128,384]{2,1,0:T(8,128)(2,1)S(1)}, bf16[8,128,384]{2,1,0:T(8,128)(2,1)}, u32[]{:S(2)}) copy-start(bf16[8,128,384]{2,1,0:T(8,128)(2,1)} %copy-done.1) | copy-start | bytes 2359300
  17.2 14.1 %copy-start = (bf16[8,200,128]{2,1,0:T(8,128)(2,1)S(1)}, bf16[8,200,128]{2,1,0:T(8,128)(2,1)}, u32[]{:S(2)}) copy-start(bf16[8,200,128]{2,1,0:T(8,128)(2,1)} %param.8) | copy-start | bytes 1228804
  17.2 14.1 %copy-start.3 = (bf16[256,512]{1,0:T(8,128)(2,1)S(1)}, bf16[256,512]{1,0:T(8,128)(2,1)}, u32[]{:S(2)}) copy-start(bf16[256,512]{1,0:T(8,128)(2,1)} %w_in_ref.1) | copy-start | bytes 786436
  17.2 14.1 %copy-start.4 = (bf16[512,128]{1,0:T(8,128)(2,1)S(1)}, bf16[512,128]{1,0:T(8,128)(2,1)}, u32[]{:S(2)}) copy-start(bf16[512,128]{1,0:T(8,128)(2,1)} %w_out_ref.1) | copy-start | bytes 393220

commit v9 on v7

--- a/solution.py
+++ b/solution.py
@@ -224,10 +224,10 @@
             weight_ref[pair, start : start + size, :] = jnp.exp2((scores - peak) * scale).astype(jnp.bfloat16)
 
     def gather(pair):
-        for block, head in enumerate(HEAD_ORDER):
-            span = slice(block * cand_count, (block + 1) * cand_count)
+        for parity in range(2):
+            span = slice(parity * head_rows // 2, (parity + 1) * head_rows // 2)
             sum_ref[pair, span, :] = jnp.dot(
-                weight_ref[pair, span, :], values[pair][head % 2], preferred_element_type=jnp.float32
+                weight_ref[pair, span, :], values[pair][parity], preferred_element_type=jnp.float32
             )
 
     def blend(pair):
@@ -273,7 +273,7 @@
         return pltpu.make_async_copy(result_ref.at[span], out_ref.at[span], sems.at[pair])
 
     stages = (score, weigh, gather, blend, enter, activate, leave)
-    begins = [pair // 2 * 5 for pair in range(pairs)]
+    begins = [pair // 2 * 5 + (pair % 2 if pair > 1 else 0) for pair in range(pairs)]
     for tick in range(len(stages) + begins[-1]):
         for pair in range(pairs):
             stage = tick - begins[pair]

time: 33.7 us -> 33.6 us (level)
  no operation moved by 1% of the time
where the time goes in v9:
time: 33.6 us; the launch traced here: 33.3 us
  blocking collectives  13.3 us (40%)
  starting transfers between devices  7.33 us (22%)
  Pallas kernels  6.41 us (19%)
  waiting for transfers between devices  5.58 us (17%)
  local copies, waits for them, and re-layouts  0.71 us (2%)
    all_to_all x1, blocking collectives, exchange(): return lax.all_to_all(parts, AXES, split_axis=0, concat_axis=0, tiled=True)  13.3 us
    all_to_all x1, starting transfers between devices, exchange(): return lax.all_to_all(parts, AXES, split_axis=0, concat_axis=0, tiled=True)  7.33 us
    all_to_all x1, waiting for transfers between devices, exchange(): return lax.all_to_all(parts, AXES, split_axis=0, concat_axis=0, tiled=True)  5.58 us
    pallas_call x1, Pallas kernels, local(): pl.pallas_call(tower_kernel, out_shape=jax.ShapeDtypeStruct((rows, width)...  3.17 us
    pallas_call x1, Pallas kernels, local(): pl.pallas_call(lambda *refs: stage_kernel(*refs, own_users=own_users), ou...  1.47 us
    pallas_call x1, Pallas kernels, local(): pl.pallas_call(distinct_kernel, out_shape=pltpu.VMEM((devices, 1, LANES),...  0.94 us
    pallas_call x1, Pallas kernels, local(): pl.pallas_call(lambda *refs: pack_kernel(*refs, own_users=own_users), out...  0.84 us
    unnamed x8, local copies, waits for them, and re-layouts  0.71 us
  transfers between devices with their start and end apart: 1, of which 1 were waited for; matrix products, arithmetic and copies ran while one was open for 0% of the time, Pallas kernels for 4%

profile of v9, /device:TPU:0, one launch (start us, length us, event | category | flops | bytes accessed | tf_op | source)
XLA Modules:
  0.0 33.3 jit_solution(6171275319417237149)
XLA Ops:
  0.0 0.0 copy-start.3
  0.0 0.7 %copy-done.3 = s32[8,200]{1,0:T(8,128)S(1)} copy-done((s32[8,200]{1,0:T(8,128)S(1)}, s32[8,200]{1,0:T(8,128)}, u32[]{:S(2)}) %copy-start.3) | copy-done | bytes 6424
  0.7 0.9 %distinct.1 = s32[32,1,128]{2,1,0:T(1,128)} custom-call(s32[8,200]{1,0:T(8,128)S(1)} %copy-done.3), custom_call_target="tpu_custom_call" | custom-call | tf_op jit(solution)/shard_map/distinct/pallas_call | solution.py:300
  1.6 7.3 %all-to-all-start = ((s32[32,1,128]{2,1,0:T(1,128)}), s32[32,1,128]{2,1,0:T(1,128)S(1)}, u32[]{:S(2)}, u32[]{:S(2)}) async-start(s32[32,1,128]{2,1,0:T(1,128)} %distinct.1), calls=%async_computation | async-start | bytes 32768 | tf_op jit(solution)/shard_map/all_to_all | solution.py:291
  9.0 1.5 %stage.1 = (bf16[20,256,128]{2,1,0:T(8,128)(2,1)S(1)}, bf16[4,800,256]{2,1,0:T(8,128)(2,1)S(1)}, f32[32,320]{1,0:T(8,128)S(1)}) custom-call(bf16[20,256,128]{2,1,0:T(8,128)(2,1)} %bitcast.6, bf16[1600,128]{1,0:T(8,128)(2,1)} %bitcast.4, s32[20,256]{1,0:T(8,128)} %bitcast.7), custom_call_target="tpu_custom_call" | custom-call | tf_op jit(solution)/shard_map/stage/pallas_call | solution.py:313
  10.4 0.0 copy-start
  10.5 0.0 copy-start.2
  10.5 5.6 %all-to-all-done.refs_0_ = s32[32,1,128]{2,1,0:T(1,128)S(1)} async-done(((s32[32,1,128]{2,1,0:T(1,128)}), s32[32,1,128]{2,1,0:T(1,128)S(1)}, u32[]{:S(2)}, u32[]{:S(2)}) %all-to-all-start) | async-done | bytes 16416 | tf_op jit(solution)/shard_map/all_to_all | solution.py:291
  16.1 0.0 copy-start.1
  16.1 0.8 %pack.1 = bf16[32,17,2,128]{3,2,1,0:T(2,128)(2,1)S(1)} custom-call(s32[32,1,128]{2,1,0:T(1,128)S(1)} %all-to-all-done.refs_0_, f32[32,320]{1,0:T(8,128)S(1)} %get-tuple-element.8.refs_1_, bf16[20,256,128]{2,1,0:T(8,128)(2,1)S(1)} %get-tuple-element.9.refs_2_), custom_call_target="tpu_custom_call" | custom-call | tf_op jit(solution)/shard_map/pack/pallas_call | solution.py:330
  16.9 13.3 %all_to_all.10.packed_ref = bf16[32,17,2,128]{3,2,1,0:T(2,128)(2,1)S(1)} all-to-all(bf16[32,17,2,128]{3,2,1,0:T(2,128)(2,1)S(1)} %pack.1), channel_id=1, replica_groups=mesh['role'=2,'shard'=16] {'role','shard'}, dimensions={0} | all-to-all | bytes 557056 | tf_op jit(solution)/shard_map/all_to_all | solution.py:291
  30.1 0.0 copy-done
  30.2 0.0 copy-done.2
  30.2 0.0 copy-done.1
  30.2 3.2 %tower.1 = bf16[1600,128]{1,0:T(8,128)(2,1)} custom-call(bf16[32,17,2,128]{3,2,1,0:T(2,128)(2,1)S(1)} %all_to_all.10.packed_ref, bf16[4,800,256]{2,1,0:T(8,128)(2,1)S(1)} %get-tuple-element.10.query_ref, bf16[1600,128]{1,0:T(8,128)(2,1)S(1)} %bitcast.5, bf16[256,512]{1,0:T(8,128)(2,1)S(1)} %copy-done.1, bf16[512,128]{1,0:T(8,128)(2,1)S(1)} %copy-done.2), custom_call_target="tpu_custom_call" | custom-call | tf_op jit(solution)/shard_map/tower/pallas_call | solution.py:340
Async XLA Ops:
  0.0 0.7 %copy-start.3 = (s32[8,200]{1,0:T(8,128)S(1)}, s32[8,200]{1,0:T(8,128)}, u32[]{:S(2)}) copy-start(s32[8,200]{1,0:T(8,128)} %cat_ref.1) | copy-start | bytes 19204
  1.6 14.4 %all-to-all-start = ((s32[32,1,128]{2,1,0:T(1,128)}), s32[32,1,128]{2,1,0:T(1,128)S(1)}, u32[]{:S(2)}, u32[]{:S(2)}) async-start(s32[32,1,128]{2,1,0:T(1,128)} %distinct.1), calls=%async_computation | async-start | bytes 32768 | tf_op jit(solution)/shard_map/all_to_all | solution.py:291
  10.4 19.7 %copy-start = (bf16[8,200,128]{2,1,0:T(8,128)(2,1)S(1)}, bf16[8,200,128]{2,1,0:T(8,128)(2,1)}, u32[]{:S(2)}) copy-start(bf16[8,200,128]{2,1,0:T(8,128)(2,1)} %param.8) | copy-start | bytes 1228804
  10.5 19.7 %copy-start.2 = (bf16[512,128]{1,0:T(8,128)(2,1)S(1)}, bf16[512,128]{1,0:T(8,128)(2,1)}, u32[]{:S(2)}) copy-start(bf16[512,128]{1,0:T(8,128)(2,1)} %w_out_ref.1) | copy-start | bytes 393220
  16.1 14.1 %copy-start.1 = (bf16[256,512]{1,0:T(8,128)(2,1)S(1)}, bf16[256,512]{1,0:T(8,128)(2,1)}, u32[]{:S(2)}) copy-start(bf16[256,512]{1,0:T(8,128)(2,1)} %w_in_ref.1) | copy-start | bytes 786436
